TPU v7x, 32 devices: a whole 2x2x4 slice. The times are simulated.
32 devices in a mesh: emb: 4 (over x, core), heads: 8 (over z, y).
Axes of the slice: x: 2, y: 2, z: 4, core: 2. Of those that a mesh axis runs over, the one named last changes fastest.
Arguments:
- hidden_in: bfloat16 [16, 8192], P(None, 'emb'), may hold values from -6 to 6
- w_z: bfloat16 [8192, 16384], P('emb', 'heads'), may hold values from -0.0625 to 0.0625
- w_x: bfloat16 [8192, 16384], P('emb', 'heads'), may hold values from -0.0625 to 0.0625
- w_bc: bfloat16 [8192, 4096], P('emb'), may hold values from -0.0625 to 0.0625
- w_dt: bfloat16 [8192, 256], P('emb', 'heads'), may hold values from -0.0625 to 0.0625
- dt_bias: float32 [256], P('heads'), may hold values from -4 to -1
- a_log: float32 [256], P('heads'), may hold values from 0 to 2.77
- skip_gain: float32 [256], P('heads'), may hold values from 0.5 to 2
- conv_x: bfloat16 [16, 3, 16384], P('emb', None, 'heads'), may hold values from -6 to 6
- conv_bc: bfloat16 [16, 3, 4096], P('emb'), may hold values from -6 to 6
- conv_wx: float32 [4, 16384], P(None, 'heads'), may hold values from -3 to 3
- conv_wbc: float32 [4, 4096], replicated, may hold values from -3 to 3
- ssm_state: float32 [16, 256, 64, 256], P('emb', 'heads'), may hold values from -0.6 to 0.6
- norm_gain: float32 [16384], P('heads'), may hold values from 0.5 to 1.5
- w_out: bfloat16 [16384, 8192], P('heads', 'emb'), may hold values from -0.046875 to 0.046875
Outputs:
- mixed: bfloat16 [16, 8192], P(None, 'emb')
- new_state: float32 [16, 256, 64, 256], P('emb', 'heads')
All inputs are finite; a program needn't handle non-finite values.
Results may differ from a plain program's by a relative error of at most 0.0051.
Values may be sent and summed in bfloat16 or wider, within the bound.
A program may use at most 128 MiB of HBM per device.

v0:
```python
import functools

import jax
import jax.numpy as jnp
from jax import lax
from jax.experimental import pallas as pl
from jax.experimental.pallas import tpu as pltpu
from jax.sharding import PartitionSpec as P

H = 256
P_SIZE = 64
N = 256
G = 8
LANES = 128
DEPTH = 6
MESH = pl.DeviceIdType.MESH
F32 = jnp.float32
BF16 = jnp.bfloat16


def silu(v):
    return v / (1.0 + jnp.exp(-v))


def softplus(v):
    return jnp.maximum(v, 0.0) + jnp.log1p(jnp.exp(-jnp.abs(v)))


def split3(v):
    high = v.astype(BF16)
    rest = v - high.astype(F32)
    mid = rest.astype(BF16)
    low = (rest - mid.astype(F32)).astype(BF16)
    return high, mid, low


def kernel(
    dims,
    hidden_hbm,
    dtb_hbm,
    alog_hbm,
    skip_hbm,
    convx_hbm,
    convwx_hbm,
    gain_hbm,
    wz_hbm,
    wx_hbm,
    wbc_hbm,
    wdt_hbm,
    convbc_hbm,
    convwbc_hbm,
    state_hbm,
    wout_hbm,
    out_ref,
    st_ref,
    hidden_ref,
    dtb_ref,
    alog_ref,
    skip_ref,
    convx_v,
    convwx_ref,
    gain_ref,
    wz_v,
    wx_v,
    wbc_v,
    wdt_v,
    convbc_v,
    convwbc_v,
    wout_v,
    xsend,
    xrecv,
    zsend,
    zrecv,
    cols_v,
    read_v,
    xc_v,
    ag_v,
    rs_send,
    rs_recv,
    fin_send,
    fin_v,
    sq_send,
    sq_recv,
    dma_sem,
    x_ss,
    x_rs,
    z_ss,
    z_rs,
    a_ss,
    a_rs,
    r_ss,
    r_rs,
    f_ss,
    f_rs,
    q_ss,
    q_rs,
):
    n_emb, n_heads, batch, bd, di, hd, cols, chunk, ochunk, fused, span = dims
    e = lax.axis_index("emb")
    h = lax.axis_index("heads")
    group = h // span

    def emb_peer(o):
        return lax.rem(e + o, n_emb)

    def head_peer(mask):
        peer = h
        bit = 1
        while bit < n_heads:
            if mask & bit:
                peer = peer + bit * (1 - 2 * lax.rem(lax.div(h, bit), 2))
            bit *= 2
        return peer

    copies = {}
    order = []

    def stream(name, src, dst):
        copies[name] = pltpu.make_async_copy(src, dst, dma_sem.at[len(order)])
        order.append(name)

    stream("hidden", hidden_hbm, hidden_ref)
    for half in range(2):
        off = pl.multiple_of(half * G * N + group * N, N)
        stream(("bc", half), wbc_hbm.at[:, pl.ds(off, N)], wbc_v.at[half])
    stream(("dt", 0), wdt_hbm, wdt_v)
    for half in range(2):
        off = pl.multiple_of(half * G * N + group * N, N)
        stream(("cb", half), convbc_hbm.at[:, :, pl.ds(off, N)], convbc_v.at[half])
        stream(("cw", half), convwbc_hbm.at[:, pl.ds(off, N)], convwbc_v.at[half])
    stream("dtb", dtb_hbm, dtb_ref)
    stream("alog", alog_hbm, alog_ref)
    stream("skip", skip_hbm, skip_ref)
    stream("convx", convx_hbm, convx_v)
    stream("convwx", convwx_hbm, convwx_ref)
    stream("gain", gain_hbm, gain_ref)
    n_chunk = di // chunk
    for c in range(n_chunk):
        stream(("x", c), wx_hbm.at[:, pl.ds(c * chunk, chunk)], wx_v.at[c])
    for c in range(n_chunk):
        stream(("z", c), wz_hbm.at[:, pl.ds(c * chunk, chunk)], wz_v.at[c])
    rows_in = min(512, di)
    for i in range(di // rows_in):
        part = pl.ds(i * rows_in, rows_in)
        stream(("s", i), state_hbm.at[:, part], st_ref.at[:, part])
    n_out = cols // ochunk
    for i in range(n_out):
        at = head_peer(n_heads - 1 - i) if fused else i
        off = pl.multiple_of(at * ochunk, ochunk)
        stream(("o", i), wout_hbm.at[:, pl.ds(off, ochunk)], wout_v.at[i])
    started = [0]

    def advance():
        if started[0] < len(order):
            copies[order[started[0]]].start()
            started[0] += 1

    def ready(name):
        copies[name].wait()
        advance()

    for _ in range(DEPTH + 12):
        advance()

    barrier = pltpu.get_barrier_semaphore()
    for o in range(1, n_emb):
        pl.semaphore_signal(barrier, inc=1, device_id={"emb": emb_peer(o)}, device_id_type=MESH)
    n_greet = n_emb - 1
    if fused:
        for o in range(1, n_heads):
            pl.semaphore_signal(
                barrier, inc=1, device_id={"heads": head_peer(o)}, device_id_type=MESH
            )
        n_greet += n_heads - 1
    elif span > 1:
        for o in range(1, span):
            pl.semaphore_signal(
                barrier,
                inc=1,
                device_id={"heads": group * span + lax.rem(h % span + o, span)},
                device_id_type=MESH,
            )
        n_greet += span - 1

    ready("hidden")
    hidden = hidden_ref[...]

    def project(weights, send, at, width):
        part = jnp.dot(hidden, weights, preferred_element_type=F32)
        for peer in range(n_emb):
            send[peer, :, at : at + width] = part[peer * bd : (peer + 1) * bd]

    heads_at = lax.broadcasted_iota(jnp.int32, (hd, di), 0)
    chans_at = lax.broadcasted_iota(jnp.int32, (hd, di), 1)
    lower = heads_at * P_SIZE
    expand = jnp.where((chans_at >= lower) & (chans_at < lower + P_SIZE), 1.0, 0.0).astype(BF16)

    k_prev = convx_v.shape[0]

    def conv_prev(values, taps):
        return sum(values[k].astype(F32) * taps[k : k + 1, :] for k in range(k_prev))

    for half in range(2):
        ready(("bc", half))
        project(wbc_v[half], xsend, di + half * N, N)
    ready(("dt", 0))
    xsend[:, :, di + 2 * N :] = jnp.zeros((n_emb, bd, LANES), F32)
    part = lax.dot_general(
        hidden, wdt_v[...], (((1,), (1,)), ((), ())), preferred_element_type=F32
    )
    for peer in range(n_emb):
        xsend[peer, :, di + 2 * N : di + 2 * N + hd] = part[peer * bd : (peer + 1) * bd]
    bc_base = []
    for half in range(2):
        ready(("cb", half))
        ready(("cw", half))
        bc_base.append(conv_prev(convbc_v.at[half], convwbc_v[half]))
    for name in ("dtb", "alog", "skip", "convx", "convwx", "gain"):
        ready(name)
    x_base = conv_prev(convx_v, convwx_ref[...])
    for c in range(n_chunk):
        ready(("x", c))
        project(wx_v[c], xsend, c * chunk, chunk)

    pl.semaphore_wait(barrier, n_greet)

    def send_emb(src, dst, ss, rs):
        made = []
        for o in range(n_emb - 1, 0, -1):
            peer = emb_peer(o)
            copy = pltpu.make_async_remote_copy(
                src_ref=src.at[peer],
                dst_ref=dst.at[o - 1],
                send_sem=ss.at[o - 1],
                recv_sem=rs.at[o - 1],
                device_id={"emb": peer},
                device_id_type=MESH,
            )
            copy.start()
            made.append(copy)
        return made

    x_copies = send_emb(xsend, xrecv, x_ss, x_rs)
    for c in range(n_chunk):
        ready(("z", c))
        project(wz_v[c], zsend, c * chunk, chunk)
    z_copies = send_emb(zsend, zrecv, z_ss, z_rs)

    for copy in x_copies:
        copy.wait_recv()
    xall = xsend[e]
    for o in range(n_emb - 1):
        xall = xall + xrecv[o]
    x_conv = silu(x_base + xall[:, 0:di] * convwx_ref[k_prev : k_prev + 1, :])
    bc = []
    for half in range(2):
        pre = xall[:, di + half * N : di + (half + 1) * N]
        bc.append(silu(bc_base[half] + pre * convwbc_v[half, k_prev : k_prev + 1, :]))
    b_group, c_group = bc
    dt_pre = xall[:, di + 2 * N : di + 2 * N + hd]
    step = softplus(dt_pre + dtb_ref[...])
    decay = jnp.exp(-jnp.exp(alog_ref[...]) * step)
    skip = jnp.broadcast_to(skip_ref[...], (bd, hd))
    by_head = jnp.concatenate([step, decay, skip], axis=0)
    by_chan = sum(jnp.dot(part, expand, preferred_element_type=F32) for part in split3(by_head))
    step_c = by_chan[0:bd]
    decay_c = by_chan[bd : 2 * bd]
    skip_c = by_chan[2 * bd : 3 * bd]
    rows = jnp.concatenate([step_c * x_conv, decay_c], axis=0)
    cols_v[...] = jnp.transpose(rows)
    xc_v[...] = skip_c * x_conv
    c_high, c_low, _ = split3(c_group)
    c_both = jnp.concatenate([c_high.astype(F32), c_low.astype(F32)], axis=0).astype(BF16)

    rows_at = min(256, rows_in)
    lane = lax.broadcasted_iota(jnp.int32, (rows_at, 2 * bd), 1)
    for i in range(di // rows_in):
        ready(("s", i))

        def update(j, carry, i=i):
            at = pl.ds(pl.multiple_of(i * rows_in + j * rows_at, rows_at), rows_at)
            found = None
            for b in range(bd):
                xcol = cols_v[at, b : b + 1]
                dcol = cols_v[at, bd + b : bd + b + 1]
                new = dcol * st_ref[b, at, :] + xcol * b_group[b : b + 1, :]
                st_ref[b, at, :] = new
                got = lax.dot_general(
                    new.astype(BF16), c_both, (((1,), (1,)), ((), ())), preferred_element_type=F32
                )
                mine = (lane == b) | (lane == bd + b)
                found = got if found is None else jnp.where(mine, got, found)
            read_v[at, :] = found
            return carry

        lax.fori_loop(0, rows_in // rows_at, update, 0)
    read_rows = jnp.transpose(read_v[...])
    read = read_rows[0:bd] + read_rows[bd : 2 * bd]

    for copy in z_copies:
        copy.wait_recv()
    zall = zsend[e]
    for o in range(n_emb - 1):
        zall = zall + zrecv[o]
    gated = (read + xc_v[...]) * silu(zall)
    total = jnp.sum(gated * gated, axis=1, keepdims=True)
    q_copies = []
    if span > 1:
        sq_send[...] = jnp.broadcast_to(total, (bd, LANES))
        for o in range(1, span):
            copy = pltpu.make_async_remote_copy(
                src_ref=sq_send,
                dst_ref=sq_recv.at[o - 1],
                send_sem=q_ss.at[o - 1],
                recv_sem=q_rs.at[o - 1],
                device_id={"heads": group * span + lax.rem(h % span + o, span)},
                device_id_type=MESH,
            )
            copy.start()
            q_copies.append(copy)
        for o, copy in enumerate(q_copies):
            copy.wait_recv()
            total = total + sq_recv[o][:, 0:1]
    inv_rms = lax.rsqrt(total / (H * P_SIZE // G) + 1e-05)
    normed = (gated * inv_rms * gain_ref[...]).astype(BF16)
    ag_v[e] = normed
    a_copies = []
    for o in range(n_emb - 1, 0, -1):
        copy = pltpu.make_async_remote_copy(
            src_ref=ag_v.at[e],
            dst_ref=ag_v.at[e],
            send_sem=a_ss.at[o - 1],
            recv_sem=a_rs.at[o - 1],
            device_id={"emb": emb_peer(o)},
            device_id_type=MESH,
        )
        copy.start()
        a_copies.append(copy)
    for copy in a_copies:
        copy.wait_recv()
    whole = jnp.concatenate([ag_v[i].astype(F32) for i in range(n_emb)], axis=0).astype(BF16)

    last = []
    own = None
    for i in range(n_out):
        ready(("o", i))
        part = jnp.dot(whole, wout_v[i], preferred_element_type=F32)
        if not fused:
            out_ref[:, i * ochunk : (i + 1) * ochunk] = part
        elif i < n_out - 1:
            rs_send[i] = part.astype(BF16)
            copy = pltpu.make_async_remote_copy(
                src_ref=rs_send.at[i],
                dst_ref=rs_recv.at[i],
                send_sem=r_ss.at[i],
                recv_sem=r_rs.at[i],
                device_id={"heads": head_peer(n_heads - 1 - i)},
                device_id_type=MESH,
            )
            copy.start()
            last.append(copy)
        else:
            own = part
    f_copies = []
    if fused:
        for i, copy in enumerate(last):
            copy.wait_recv()
            own = own + rs_recv[i].astype(F32)
        fin_send[...] = own.astype(BF16)
        for o in range(n_heads - 1, 0, -1):
            copy = pltpu.make_async_remote_copy(
                src_ref=fin_send,
                dst_ref=fin_v.at[h],
                send_sem=f_ss.at[o - 1],
                recv_sem=f_rs.at[o - 1],
                device_id={"heads": head_peer(o)},
                device_id_type=MESH,
            )
            copy.start()
            f_copies.append(copy)
        fin_v[h] = fin_send[...]
        for copy in f_copies:
            copy.wait_recv()
        for i in range(n_heads):
            out_ref[:, i * ochunk : (i + 1) * ochunk] = fin_v[i]
    for copy in x_copies + z_copies + q_copies + a_copies + last + f_copies:
        copy.wait_send()


def in_hbm(*arrays):
    return [pltpu.with_memory_space_constraint(array, pltpu.HBM) for array in arrays]


def on_device(
    hidden_in,
    w_z,
    w_x,
    w_bc,
    w_dt,
    dt_bias,
    a_log,
    skip_gain,
    conv_x,
    conv_bc,
    conv_wx,
    conv_wbc,
    ssm_state,
    norm_gain,
    w_out,
):
    n_emb = lax.axis_size("emb")
    n_heads = lax.axis_size("heads")
    span = n_heads // G
    batch, depth = hidden_in.shape
    bd = conv_x.shape[0]
    k_prev = conv_x.shape[1]
    di = w_x.shape[1]
    hd = w_dt.shape[1]
    cols = w_out.shape[1]
    fused = cols % (n_heads * LANES) == 0
    chunk = min(512, di)
    ochunk = cols // n_heads if fused else min(256, cols)
    dims = (n_emb, n_heads, batch, bd, di, hd, cols, chunk, ochunk, fused, span)
    n_chunk = di // chunk
    n_out = cols // ochunk
    x_cols = di + 2 * N + LANES
    n_streams = 14 + 2 * n_chunk + di // min(512, di) + n_out
    vm = pl.BlockSpec(memory_space=pltpu.VMEM)
    hbm = pl.BlockSpec(memory_space=pltpu.HBM)
    dma = pltpu.SemaphoreType.DMA
    rs_n = max(n_heads - 1, 1) if fused else 1
    rs_shape = (batch, ochunk) if fused else (batch, LANES)
    fin_n = n_heads if fused else 1
    e_n = max(n_emb - 1, 1)
    q_n = max(span - 1, 1)
    out, new_state = pl.pallas_call(
        functools.partial(kernel, dims),
        out_shape=(
            jax.ShapeDtypeStruct((batch, cols), BF16 if fused else F32),
            pltpu.VMEM((bd, di, N), F32),
        ),
        in_specs=[hbm] * 15,
        out_specs=(vm, vm),
        scratch_shapes=[
            pltpu.VMEM((batch, depth), BF16),
            pltpu.VMEM((1, hd), F32),
            pltpu.VMEM((1, hd), F32),
            pltpu.VMEM((1, hd), F32),
            pltpu.VMEM((k_prev, bd, di), BF16),
            pltpu.VMEM((k_prev + 1, di), F32),
            pltpu.VMEM((1, di), F32),
            pltpu.VMEM((n_chunk, depth, chunk), BF16),
            pltpu.VMEM((n_chunk, depth, chunk), BF16),
            pltpu.VMEM((2, depth, N), BF16),
            pltpu.VMEM((hd, depth), BF16),
            pltpu.VMEM((2, k_prev, bd, N), BF16),
            pltpu.VMEM((2, k_prev + 1, N), F32),
            pltpu.VMEM((n_out, w_out.shape[0], ochunk), BF16),
            pltpu.VMEM((n_emb, bd, x_cols), F32),
            pltpu.VMEM((e_n, bd, x_cols), F32),
            pltpu.VMEM((n_emb, bd, di), F32),
            pltpu.VMEM((e_n, bd, di), F32),
            pltpu.VMEM((di, 2 * bd), F32),
            pltpu.VMEM((di, 2 * bd), F32),
            pltpu.VMEM((bd, di), F32),
            pltpu.VMEM((n_emb, bd, di), BF16),
            pltpu.VMEM((rs_n,) + rs_shape, BF16),
            pltpu.VMEM((rs_n,) + rs_shape, BF16),
            pltpu.VMEM(rs_shape, BF16),
            pltpu.VMEM((fin_n,) + rs_shape, BF16),
            pltpu.VMEM((bd, LANES), F32),
            pltpu.VMEM((q_n, bd, LANES), F32),
            dma((n_streams,)),
            dma((e_n,)),
            dma((e_n,)),
            dma((e_n,)),
            dma((e_n,)),
            dma((e_n,)),
            dma((e_n,)),
            dma((rs_n,)),
            dma((rs_n,)),
            dma((rs_n,)),
            dma((rs_n,)),
            dma((q_n,)),
            dma((q_n,)),
        ],
        compiler_params=pltpu.CompilerParams(
            collective_id=0, has_side_effects=True, vmem_limit_bytes=44 * 1024 * 1024
        ),
    )(
        *in_hbm(
        hidden_in,
        dt_bias.reshape(1, hd),
        a_log.reshape(1, hd),
        skip_gain.reshape(1, hd),
        jnp.transpose(conv_x, (1, 0, 2)),
        conv_wx,
        norm_gain.reshape(1, di),
        w_z,
        w_x,
        w_bc,
        w_dt.T,
        jnp.transpose(conv_bc, (1, 0, 2)),
        conv_wbc,
        ssm_state.reshape(bd, di, N),
        w_out,
        )
    )
    mixed = out if fused else lax.psum(out, "heads").astype(BF16)
    return (mixed, new_state.reshape(bd, hd, P_SIZE, N))


def solution(mesh):
    in_specs = (
        P(None, "emb"),
        P("emb", "heads"),
        P("emb", "heads"),
        P("emb", None),
        P("emb", "heads"),
        P("heads"),
        P("heads"),
        P("heads"),
        P("emb", None, "heads"),
        P("emb", None, None),
        P(None, "heads"),
        P(),
        P("emb", "heads", None, None),
        P("heads"),
        P("heads", "emb"),
    )
    out_specs = (P(None, "emb"), P("emb", "heads", None, None))
    return jax.shard_map(
        on_device, mesh=mesh, in_specs=in_specs, out_specs=out_specs, check_vma=False
    )
```

profile of v0, /device:TPU:0, one launch (start us, length us, event | category | flops | bytes accessed | tf_op | source)
XLA Modules:
  0.0 34.6 jit_solution(17921242407619379135)
XLA Ops:
  0.6 29.9 %shard_map.158 = (bf16[16,2048]{1,0:T(8,128)(2,1)S(1)}, f32[4,2048,256]{2,1,0:T(8,128)S(1)}) custom-call(bf16[16,2048]{1,0:T(8,128)(2,1)} %hidden_hbm.1, f32[1,32]{1,0:T(1,128)} %bitcast.15, f32[1,32]{1,0:T(1,128)} %bitcast.16, f32[1,32]{1,0:T(1,128)} %bitcast.17, bf16[3,4,2048]{2,1,0:T(4,128)(2,1)} %bitcast.13, f32[4,2048]{1,0:T(4,128)} %convwx_hbm.1, ...), custom_call_target="tpu_custom_call" | custom-call | tf_op jit(solution)/shard_map/pallas_call | solution.py:436
  30.6 3.4 %copy.19 = f32[4,32,64,256]{3,2,1,0:T(8,128)} copy(f32[4,32,64,256]{3,2,1,0:T(8,128)S(1)} %bitcast.9) | data formatting | bytes 16777216
  34.0 0.6 %copy.20 = bf16[16,2048]{1,0:T(8,128)(2,1)} copy(bf16[16,2048]{1,0:T(8,128)(2,1)S(1)} %get-tuple-element.10) | data formatting | bytes 131072
where the time goes:
time: 34.8 us; the launch traced here: 34.6 us
  Pallas kernels  29.9 us (86%)
  local copies, waits for them, and re-layouts  4.03 us (12%)
  between operations  0.64 us (2%)
    pallas_call x1, Pallas kernels, on_device(): pl.pallas_call(functools.partial(kernel, dims), out_shape=(jax.ShapeDtype...  29.9 us
    unnamed x2, local copies, waits for them, and re-layouts  4.03 us

commit v1 on v0

v1 whole, which is shorter than its diff:
```python
import functools

import jax
import jax.numpy as jnp
from jax import lax
from jax.experimental import pallas as pl
from jax.experimental.pallas import tpu as pltpu
from jax.sharding import PartitionSpec as P

H = 256
P_SIZE = 64
N = 256
G = 8
LANES = 128
DEPTH = 18
MESH = pl.DeviceIdType.MESH
F32 = jnp.float32
BF16 = jnp.bfloat16


def silu(v):
    return v / (1.0 + jnp.exp(-v))


def softplus(v):
    return jnp.maximum(v, 0.0) + jnp.log1p(jnp.exp(-jnp.abs(v)))


def split3(v):
    high = v.astype(BF16)
    rest = v - high.astype(F32)
    mid = rest.astype(BF16)
    low = (rest - mid.astype(F32)).astype(BF16)
    return high, mid, low


def kernel(
    dims,
    hidden_hbm,
    dtb_hbm,
    alog_hbm,
    skip_hbm,
    convx_hbm,
    convwx_hbm,
    gain_hbm,
    wz_hbm,
    wx_hbm,
    wbc_hbm,
    wdt_hbm,
    convbc_hbm,
    convwbc_hbm,
    state_hbm,
    wout_hbm,
    out_ref,
    st_ref,
    hidden_ref,
    dtb_ref,
    alog_ref,
    skip_ref,
    convx_v,
    convwx_ref,
    gain_ref,
    wz_v,
    wx_v,
    wbc_v,
    wdt_v,
    convbc_v,
    convwbc_v,
    wout_v,
    bpart,
    bsend,
    brecv,
    dsend,
    drecv,
    xpart,
    xsend,
    xrecv,
    zpart,
    zsend,
    zrecv,
    cols_v,
    xc_v,
    ag_v,
    ss_v,
    acc_v,
    rs_send,
    rs_recv,
    fin_send,
    fin_v,
    sq_send,
    sq_recv,
    dma_sem,
    send_sem,
    recv_sem,
):
    (n_emb, n_heads, batch, bd, di, hd, cols, chunk, ochunk, fused, span) = dims
    e = lax.axis_index("emb")
    h = lax.axis_index("heads")
    group = h // span
    n_chunk = di // chunk

    def emb_peer(o):
        return lax.rem(e + o, n_emb)

    def head_peer(mask):
        peer = h
        bit = 1
        while bit < n_heads:
            if mask & bit:
                peer = peer + bit * (1 - 2 * lax.rem(lax.div(h, bit), 2))
            bit *= 2
        return peer

    copies = {}
    order = []

    def stream(name, src, dst):
        copies[name] = pltpu.make_async_copy(src, dst, dma_sem.at[len(order)])
        order.append(name)

    stream("hidden", hidden_hbm, hidden_ref)
    for half in range(2):
        off = pl.multiple_of(half * G * N + group * N, N)
        stream(
            ("bc", half), wbc_hbm.at[:, pl.ds(off, N)], wbc_v.at[:, half * N : (half + 1) * N]
        )
    stream("dt", wdt_hbm, wdt_v)
    for c in range(n_chunk):
        stream(("x", c), wx_hbm.at[:, pl.ds(c * chunk, chunk)], wx_v.at[c])
    for half in range(2):
        off = pl.multiple_of(half * G * N + group * N, N)
        stream(("cb", half), convbc_hbm.at[:, :, pl.ds(off, N)], convbc_v.at[half])
        stream(("cw", half), convwbc_hbm.at[:, pl.ds(off, N)], convwbc_v.at[half])
    stream("dtb", dtb_hbm, dtb_ref)
    stream("alog", alog_hbm, alog_ref)
    stream("skip", skip_hbm, skip_ref)
    stream("convx", convx_hbm, convx_v)
    stream("convwx", convwx_hbm, convwx_ref)
    stream("gain", gain_hbm, gain_ref)
    for c in range(n_chunk):
        stream(("z", c), wz_hbm.at[:, pl.ds(c * chunk, chunk)], wz_v.at[c])
    for c in range(n_chunk):
        part = pl.ds(c * chunk, chunk)
        stream(("s", c), state_hbm.at[:, part], st_ref.at[:, part])
    for c in range(n_chunk):
        stream(("o", c), wout_hbm.at[pl.ds(c * chunk, chunk)], wout_v.at[c])
    started = [0]

    def advance():
        if started[0] < len(order):
            copies[order[started[0]]].start()
            started[0] += 1

    def ready(name):
        with jax.named_scope("W_" + (name if isinstance(name, str) else name[0] + str(name[1]))):
            copies[name].wait()
        advance()

    for _ in range(DEPTH):
        advance()

    barrier = pltpu.get_barrier_semaphore()
    for o in range(1, n_emb):
        pl.semaphore_signal(barrier, inc=1, device_id={"emb": emb_peer(o)}, device_id_type=MESH)
    n_greet = n_emb - 1
    if fused:
        for o in range(1, n_heads):
            pl.semaphore_signal(
                barrier, inc=1, device_id={"heads": head_peer(o)}, device_id_type=MESH
            )
        n_greet += n_heads - 1
    elif span > 1:
        for o in range(1, span):
            pl.semaphore_signal(
                barrier,
                inc=1,
                device_id={"heads": group * span + lax.rem(h % span + o, span)},
                device_id_type=MESH,
            )
        n_greet += span - 1

    made = []

    def send(src, dst, where):
        at = len(made)
        copy = pltpu.make_async_remote_copy(
            src_ref=src,
            dst_ref=dst,
            send_sem=send_sem.at[at],
            recv_sem=recv_sem.at[at],
            device_id=where,
            device_id_type=MESH,
        )
        copy.start()
        made.append(copy)
        return copy

    def send_emb(src, dst):
        sent = []
        for o in range(n_emb - 1, 0, -1):
            peer = emb_peer(o)
            sent.append(send(src.at[peer], dst.at[o - 1], {"emb": peer}))
        return sent

    def arrived(group_of, name):
        for copy in group_of:
            with jax.named_scope(name):
                copy.wait_recv()

    heads_at = lax.broadcasted_iota(jnp.int32, (hd, di), 0)
    chans_at = lax.broadcasted_iota(jnp.int32, (hd, di), 1)
    lower = heads_at * P_SIZE
    expand = jnp.where((chans_at >= lower) & (chans_at < lower + P_SIZE), 1.0, 0.0).astype(BF16)

    ready("hidden")
    hidden = hidden_ref[...]

    def project(weights, own, out):
        part = jnp.dot(hidden, weights, preferred_element_type=F32)
        for peer in range(n_emb):
            mine = part[peer * bd : (peer + 1) * bd]
            own[peer] = mine
            out[peer] = mine.astype(BF16)

    k_prev = convx_v.shape[0]

    def conv_prev(values, taps):
        return sum(values[k].astype(F32) * taps[k : k + 1, :] for k in range(k_prev))

    for half in range(2):
        ready(("bc", half))
    project(wbc_v[...], bpart, bsend)
    ready("dt")
    dsend[...] = jnp.zeros(dsend.shape, F32)
    part = lax.dot_general(
        hidden, wdt_v[...], (((1,), (1,)), ((), ())), preferred_element_type=F32
    )
    for peer in range(n_emb):
        dsend[peer, :, 0:hd] = part[peer * bd : (peer + 1) * bd]

    greet_at = min(2, n_chunk)
    x_copies = []
    for c in range(n_chunk):
        if c == greet_at:
            with jax.named_scope("BARRIER"):
                pl.semaphore_wait(barrier, n_greet)
            b_copies = send_emb(bsend, brecv)
            d_copies = send_emb(dsend, drecv)
            for k in range(c):
                x_copies.append(send_emb(xsend.at[k], xrecv.at[k]))
        ready(("x", c))
        project(wx_v[c], xpart.at[c], xsend.at[c])
        if c >= greet_at:
            x_copies.append(send_emb(xsend.at[c], xrecv.at[c]))
    if greet_at >= n_chunk:
        pl.semaphore_wait(barrier, n_greet)
        b_copies = send_emb(bsend, brecv)
        d_copies = send_emb(dsend, drecv)
        for k in range(n_chunk):
            x_copies.append(send_emb(xsend.at[k], xrecv.at[k]))

    z_copies = []

    def do_z(c):
        ready(("z", c))
        project(wz_v[c], zpart.at[c], zsend.at[c])
        z_copies.append(send_emb(zsend.at[c], zrecv.at[c]))

    def total_of(own, got):
        value = own[e]
        for o in range(n_emb - 1):
            value = value + got[o].astype(F32)
        return value

    bc_base = []
    for half in range(2):
        ready(("cb", half))
        ready(("cw", half))
        bc_base.append(conv_prev(convbc_v.at[half], convwbc_v[half]))
    for name in ("dtb", "alog", "skip", "convx", "convwx", "gain"):
        ready(name)

    early = max(n_chunk - 2, 0)
    for c in range(early):
        do_z(c)

    arrived(b_copies, "BRECV")
    arrived(d_copies, "DRECV")
    b_all = total_of(bpart, brecv)
    bc = []
    for half in range(2):
        pre = b_all[:, half * N : (half + 1) * N]
        bc.append(silu(bc_base[half] + pre * convwbc_v[half, k_prev : k_prev + 1, :]))
    b_group, c_group = bc
    c_high, c_low, _ = split3(c_group)
    c_both = jnp.concatenate([c_high.astype(F32), c_low.astype(F32)], axis=0).astype(BF16)
    b_dot_c = jnp.sum(b_group * c_group, axis=1, keepdims=True)
    dt_pre = total_of(dsend, drecv)[:, 0:hd]
    step = softplus(dt_pre + dtb_ref[...])
    decay = jnp.exp(-jnp.exp(alog_ref[...]) * step)
    skip = jnp.broadcast_to(skip_ref[...], (bd, hd))
    by_head = jnp.concatenate([step, decay, skip], axis=0)
    by_chan = sum(jnp.dot(part, expand, preferred_element_type=F32) for part in split3(by_head))
    step_c = by_chan[0:bd]
    decay_c = by_chan[bd : 2 * bd]
    skip_c = by_chan[2 * bd : 3 * bd]

    for c in range(early, n_chunk - 1):
        do_z(c)

    for c in range(n_chunk):
        arrived(x_copies[c], "XRECV")
        here = slice(c * chunk, (c + 1) * chunk)
        x_base = conv_prev(convx_v.at[:, :, here], convwx_ref[:, here])
        x_all = total_of(xpart.at[c], xrecv.at[c])
        x_conv = silu(x_base + x_all * convwx_ref[k_prev : k_prev + 1, here])
        push = step_c[:, here] * x_conv
        rows = jnp.concatenate([push, decay_c[:, here]], axis=0)
        cols_v[here, :] = jnp.transpose(rows)
        xc_v[:, here] = skip_c[:, here] * x_conv + push * b_dot_c
    do_z(n_chunk - 1)

    rows_at = min(256, chunk)
    row = lax.broadcasted_iota(jnp.int32, (2 * bd, chunk), 0)
    raws = []

    def readout(c):
        found = None
        for b in range(bd):
            got = lax.dot_general(
                c_both,
                st_ref[b, c * chunk : (c + 1) * chunk, :].astype(BF16),
                (((1,), (1,)), ((), ())),
                preferred_element_type=F32,
            )
            mine = (row == b) | (row == bd + b)
            found = got if found is None else jnp.where(mine, got, found)
        raws.append(found[0:bd] + found[bd : 2 * bd])

    def update(c):
        def step_of(j, carry):
            at = pl.ds(pl.multiple_of(c * chunk + j * rows_at, rows_at), rows_at)
            for b in range(bd):
                xcol = cols_v[at, b : b + 1]
                dcol = cols_v[at, bd + b : bd + b + 1]
                st_ref[b, at, :] = dcol * st_ref[b, at, :] + xcol * b_group[b : b + 1, :]
            return carry

        with jax.named_scope("UPD"):
            lax.fori_loop(0, chunk // rows_at, step_of, 0)

    late = n_chunk // 2
    for c in range(n_chunk):
        ready(("s", c))
        readout(c)
        if c < late:
            update(c)

    a_copies = []
    total = None
    for c in range(n_chunk):
        arrived(z_copies[c], "ZRECV")
        here = slice(c * chunk, (c + 1) * chunk)
        z_all = total_of(zpart.at[c], zrecv.at[c])
        read = decay_c[:, here] * raws[c] + xc_v[:, here]
        gated = read * silu(z_all)
        squares = jnp.sum(gated * gated, axis=1, keepdims=True)
        total = squares if total is None else total + squares
        ag_v[c, e] = (gated * gain_ref[:, here]).astype(BF16)
        sent = []
        for o in range(n_emb - 1, 0, -1):
            sent.append(send(ag_v.at[c, e], ag_v.at[c, e], {"emb": emb_peer(o)}))
        a_copies.append(sent)
    q_copies = []
    if span > 1:
        sq_send[...] = jnp.broadcast_to(total, (bd, LANES))
        for o in range(1, span):
            q_copies.append(
                send(
                    sq_send,
                    sq_recv.at[o - 1],
                    {"heads": group * span + lax.rem(h % span + o, span)},
                )
            )
        for o, copy in enumerate(q_copies):
            copy.wait_recv()
            total = total + sq_recv[o][:, 0:1]
    ss_v[e] = jnp.broadcast_to(total, (bd, LANES))
    s_copies = []
    for o in range(n_emb - 1, 0, -1):
        s_copies.append(send(ss_v.at[e], ss_v.at[e], {"emb": emb_peer(o)}))

    for c in range(late, n_chunk):
        update(c)

    acc = None
    for c in range(n_chunk):
        arrived(a_copies[c], "ARECV")
        whole = jnp.concatenate([ag_v[c, i].astype(F32) for i in range(n_emb)], axis=0).astype(BF16)
        ready(("o", c))
        part = jnp.dot(whole, wout_v[c], preferred_element_type=F32)
        acc = part if acc is None else acc + part
    arrived(s_copies, "SRECV")
    sums = jnp.concatenate([ss_v[i] for i in range(n_emb)], axis=0)[:, 0:1]
    inv_rms = lax.rsqrt(sums / (H * P_SIZE // G) + 1e-05)
    acc = acc * inv_rms
    if not fused:
        out_ref[...] = acc
    else:
        acc_v[...] = acc
        last = []
        for i in range(n_heads - 1):
            peer = head_peer(n_heads - 1 - i)
            at = pl.ds(pl.multiple_of(peer * ochunk, ochunk), ochunk)
            rs_send[i] = acc_v[:, at].astype(BF16)
            last.append(send(rs_send.at[i], rs_recv.at[i], {"heads": peer}))
        own = acc_v[:, pl.ds(pl.multiple_of(h * ochunk, ochunk), ochunk)]
        for i, copy in enumerate(last):
            with jax.named_scope("RRECV"):
                copy.wait_recv()
            own = own + rs_recv[i].astype(F32)
        fin_send[...] = own.astype(BF16)
        f_copies = []
        for o in range(n_heads - 1, 0, -1):
            f_copies.append(send(fin_send, fin_v.at[h], {"heads": head_peer(o)}))
        out_ref[h] = fin_send[...]
        for i, copy in enumerate(f_copies):
            with jax.named_scope("FRECV"):
                copy.wait_recv()
        for i in range(1, n_heads):
            peer = head_peer(i)
            out_ref[peer] = fin_v[peer]
    with jax.named_scope("SENT"):
        for copy in made:
            copy.wait_send()


def write_kernel(n_parts, n_heads, ochunk, has_out, *refs):
    if has_out:
        st_v, fin_v, st_hbm, out_hbm, sem = refs
    else:
        st_v, st_hbm, sem = refs
    made = []
    if has_out:
        for i in range(n_heads):
            made.append(
                pltpu.make_async_copy(
                    fin_v.at[i],
                    out_hbm.at[:, i * ochunk : (i + 1) * ochunk],
                    sem.at[i],
                )
            )
            made[-1].start()
    bd, di, _ = st_v.shape
    rows = di // n_parts
    for b in range(bd):
        for i in range(n_parts):
            part = pl.ds(i * rows, rows)
            made.append(
                pltpu.make_async_copy(
                    st_v.at[b, part], st_hbm.at[b, part], sem.at[n_heads + b * n_parts + i]
                )
            )
            made[-1].start()
    for copy in made:
        copy.wait()


def in_hbm(*arrays):
    return [pltpu.with_memory_space_constraint(array, pltpu.HBM) for array in arrays]


def on_device(
    hidden_in,
    w_z,
    w_x,
    w_bc,
    w_dt,
    dt_bias,
    a_log,
    skip_gain,
    conv_x,
    conv_bc,
    conv_wx,
    conv_wbc,
    ssm_state,
    norm_gain,
    w_out,
):
    n_emb = lax.axis_size("emb")
    n_heads = lax.axis_size("heads")
    span = n_heads // G
    batch, depth = hidden_in.shape
    bd = conv_x.shape[0]
    k_prev = conv_x.shape[1]
    di = w_x.shape[1]
    hd = w_dt.shape[1]
    cols = w_out.shape[1]
    fused = cols % (n_heads * LANES) == 0
    chunk = min(512, di)
    ochunk = cols // n_heads if fused else cols
    dims = (n_emb, n_heads, batch, bd, di, hd, cols, chunk, ochunk, fused, span)
    n_chunk = di // chunk
    n_streams = 14 + 4 * n_chunk
    vm = pl.BlockSpec(memory_space=pltpu.VMEM)
    hbm = pl.BlockSpec(memory_space=pltpu.HBM)
    dma = pltpu.SemaphoreType.DMA
    rs_n = max(n_heads - 1, 1) if fused else 1
    rs_shape = (batch, ochunk) if fused else (batch, LANES)
    fin_n = n_heads if fused else 1
    e_n = max(n_emb - 1, 1)
    q_n = max(span - 1, 1)
    n_remote = (3 + 3 * n_chunk) * e_n + q_n + 2 * rs_n
    out_shape = (n_heads, batch, ochunk) if fused else (batch, cols)
    out, new_state = pl.pallas_call(
        functools.partial(kernel, dims),
        out_shape=(
            pltpu.VMEM(out_shape, BF16 if fused else F32),
            pltpu.VMEM((bd, di, N), F32),
        ),
        in_specs=[hbm] * 15,
        out_specs=(vm, vm),
        scratch_shapes=[
            pltpu.VMEM((batch, depth), BF16),
            pltpu.VMEM((1, hd), F32),
            pltpu.VMEM((1, hd), F32),
            pltpu.VMEM((1, hd), F32),
            pltpu.VMEM((k_prev, bd, di), BF16),
            pltpu.VMEM((k_prev + 1, di), F32),
            pltpu.VMEM((1, di), F32),
            pltpu.VMEM((n_chunk, depth, chunk), BF16),
            pltpu.VMEM((n_chunk, depth, chunk), BF16),
            pltpu.VMEM((depth, 2 * N), BF16),
            pltpu.VMEM((hd, depth), BF16),
            pltpu.VMEM((2, k_prev, bd, N), BF16),
            pltpu.VMEM((2, k_prev + 1, N), F32),
            pltpu.VMEM((n_chunk, chunk, cols), BF16),
            pltpu.VMEM((n_emb, bd, 2 * N), F32),
            pltpu.VMEM((n_emb, bd, 2 * N), BF16),
            pltpu.VMEM((e_n, bd, 2 * N), BF16),
            pltpu.VMEM((n_emb, bd, LANES), F32),
            pltpu.VMEM((e_n, bd, LANES), F32),
            pltpu.VMEM((n_chunk, n_emb, bd, chunk), F32),
            pltpu.VMEM((n_chunk, n_emb, bd, chunk), BF16),
            pltpu.VMEM((n_chunk, e_n, bd, chunk), BF16),
            pltpu.VMEM((n_chunk, n_emb, bd, chunk), F32),
            pltpu.VMEM((n_chunk, n_emb, bd, chunk), BF16),
            pltpu.VMEM((n_chunk, e_n, bd, chunk), BF16),
            pltpu.VMEM((di, 2 * bd), F32),
            pltpu.VMEM((bd, di), F32),
            pltpu.VMEM((n_chunk, n_emb, bd, chunk), BF16),
            pltpu.VMEM((n_emb, bd, LANES), F32),
            pltpu.VMEM((batch, cols), F32),
            pltpu.VMEM((rs_n,) + rs_shape, BF16),
            pltpu.VMEM((rs_n,) + rs_shape, BF16),
            pltpu.VMEM(rs_shape, BF16),
            pltpu.VMEM((fin_n,) + rs_shape, BF16),
            pltpu.VMEM((bd, LANES), F32),
            pltpu.VMEM((q_n, bd, LANES), F32),
            dma((n_streams,)),
            dma((n_remote,)),
            dma((n_remote,)),
        ],
        compiler_params=pltpu.CompilerParams(
            collective_id=0, has_side_effects=True, vmem_limit_bytes=48 * 1024 * 1024
        ),
    )(
        *in_hbm(
            hidden_in,
            dt_bias.reshape(1, hd),
            a_log.reshape(1, hd),
            skip_gain.reshape(1, hd),
            jnp.transpose(conv_x, (1, 0, 2)),
            conv_wx,
            norm_gain.reshape(1, di),
            w_z,
            w_x,
            w_bc,
            w_dt.T,
            jnp.transpose(conv_bc, (1, 0, 2)),
            conv_wbc,
            ssm_state.reshape(bd, di, N),
            w_out,
        )
    )
    n_parts = max(di // 512, 1)
    params = pltpu.CompilerParams(vmem_limit_bytes=2 * 1024 * 1024)
    sems = dma((n_heads + bd * n_parts,))
    state_shape = jax.ShapeDtypeStruct((bd, di, N), F32)
    write = functools.partial(write_kernel, n_parts, n_heads, ochunk, fused)
    if fused:
        new_state, mixed = pl.pallas_call(
            write,
            out_shape=(state_shape, jax.ShapeDtypeStruct((batch, cols), BF16)),
            in_specs=[vm, vm],
            out_specs=(hbm, hbm),
            scratch_shapes=[sems],
            compiler_params=params,
        )(new_state, out)
    else:
        new_state = pl.pallas_call(
            write,
            out_shape=state_shape,
            in_specs=[vm],
            out_specs=hbm,
            scratch_shapes=[sems],
            compiler_params=params,
        )(new_state)
        mixed = lax.psum(out, "heads").astype(BF16)
    return (mixed, new_state.reshape(bd, hd, P_SIZE, N))


def solution(mesh):
    in_specs = (
        P(None, "emb"),
        P("emb", "heads"),
        P("emb", "heads"),
        P("emb", None),
        P("emb", "heads"),
        P("heads"),
        P("heads"),
        P("heads"),
        P("emb", None, "heads"),
        P("emb", None, None),
        P(None, "heads"),
        P(),
        P("emb", "heads", None, None),
        P("heads"),
        P("heads", "emb"),
    )
    out_specs = (P(None, "emb"), P("emb", "heads", None, None))
    return jax.shard_map(
        on_device, mesh=mesh, in_specs=in_specs, out_specs=out_specs, check_vma=False
    )
```

time: 34.8 us -> 32 us (0.920)
  local copies, waits for them, and re-layouts: 4.03 us -> 0 us
  Pallas kernels: 29.9 us -> 31.2 us
    unnamed x2 -> x0, local copies, waits for them, and re-layouts: 4.03 us -> none
    pallas_call x1 -> x2, Pallas kernels: 29.9 us -> 31.2 us  [the longest x1 27.7 us: on_device(): pl.pallas_call(functools.partial(kernel, dims), out_shape=(pltpu.VMEM(out...]
where the time goes in v1:
time: 32 us; the launch traced here: 31.8 us
  Pallas kernels  31.2 us (98%)
  between operations  0.64 us (2%)
    pallas_call x1, Pallas kernels, on_device(): pl.pallas_call(functools.partial(kernel, dims), out_shape=(pltpu.VMEM(out...  27.7 us
    pallas_call x1, Pallas kernels, on_device(): pl.pallas_call(write, out_shape=(state_shape, jax.ShapeDtypeStruct((batch...  3.52 us

profile of v1, /device:TPU:0, one launch (start us, length us, event | category | flops | bytes accessed | tf_op | source)
XLA Modules:
  0.0 31.8 jit_solution(18117398432186196640)
XLA Ops:
  0.6 27.7 %shard_map.158 = (bf16[8,16,256]{2,1,0:T(8,128)(2,1)S(1)}, f32[4,2048,256]{2,1,0:T(8,128)S(1)}) custom-call(bf16[16,2048]{1,0:T(8,128)(2,1)} %hidden_hbm.1, f32[1,32]{1,0:T(1,128)} %bitcast.14, f32[1,32]{1,0:T(1,128)} %bitcast.15, f32[1,32]{1,0:T(1,128)} %bitcast.16, bf16[3,4,2048]{2,1,0:T(4,128)(2,1)} %bitcast.12, f32[4,2048]{1,0:T(4,128)} %convwx_hbm.1, ...), custom_call_target="tpu_custom_call" | custom-call | tf_op jit(solution)/shard_map/pallas_call | solution.py:515
  28.3 3.5 %shard_map.159 = (f32[4,2048,256]{2,1,0:T(8,128)}, bf16[16,2048]{1,0:T(8,128)(2,1)}) custom-call(f32[4,2048,256]{2,1,0:T(8,128)S(1)} %get-tuple-element.6.refs_0_, bf16[8,16,256]{2,1,0:T(8,128)(2,1)S(1)} %get-tuple-element.7.refs_1_), custom_call_target="tpu_custom_call" | custom-call | tf_op jit(solution)/shard_map/pallas_call | solution.py:592

commit v2 on v1

--- a/solution.py
+++ b/solution.py
@@ -13,6 +13,8 @@
 G = 8
 LANES = 128
 DEPTH = 18
+EARLY = 1
+GROUPS = ("bc", "dt", "x", "z", "ss", "sq", "rs", "ag")
 MESH = pl.DeviceIdType.MESH
 F32 = jnp.float32
 BF16 = jnp.bfloat16
@@ -79,25 +81,27 @@
     zsend,
     zrecv,
     cols_v,
-    xc_v,
     ag_v,
     ss_v,
-    acc_v,
     rs_send,
     rs_recv,
     fin_send,
-    fin_v,
     sq_send,
     sq_recv,
     dma_sem,
     send_sem,
     recv_sem,
 ):
-    (n_emb, n_heads, batch, bd, di, hd, cols, chunk, ochunk, fused, span) = dims
+    (n_emb, n_heads, batch, bd, di, hd, cols, chunk, n_own, fused, span) = dims
     e = lax.axis_index("emb")
     h = lax.axis_index("heads")
     group = h // span
     n_chunk = di // chunk
+    e_n = n_emb - 1
+    core = lax.rem(e, 2)
+    first_own = n_heads // 4
+    in_middle = (h >= first_own) & (h < first_own + n_own)
+    owner = (core == 1) & in_middle
 
     def emb_peer(o):
         return lax.rem(e + o, n_emb)
@@ -111,12 +115,11 @@
             bit *= 2
         return peer
 
-    copies = {}
-    order = []
+    queue = []
+    running = {}
 
     def stream(name, src, dst):
-        copies[name] = pltpu.make_async_copy(src, dst, dma_sem.at[len(order)])
-        order.append(name)
+        queue.append((name, src, dst))
 
     stream("hidden", hidden_hbm, hidden_ref)
     for half in range(2):
@@ -144,20 +147,20 @@
         stream(("s", c), state_hbm.at[:, part], st_ref.at[:, part])
     for c in range(n_chunk):
         stream(("o", c), wout_hbm.at[pl.ds(c * chunk, chunk)], wout_v.at[c])
-    started = [0]
-
-    def advance():
-        if started[0] < len(order):
-            copies[order[started[0]]].start()
-            started[0] += 1
+    def advance(slot):
+        if queue:
+            name, src, dst = queue.pop(0)
+            running[name] = (pltpu.make_async_copy(src, dst, dma_sem.at[slot]), slot)
+            running[name][0].start()
 
     def ready(name):
+        copy, slot = running[name]
         with jax.named_scope("W_" + (name if isinstance(name, str) else name[0] + str(name[1]))):
-            copies[name].wait()
-        advance()
-
-    for _ in range(DEPTH):
-        advance()
+            copy.wait()
+        advance(slot)
+
+    for slot in range(DEPTH):
+        advance(slot)
 
     barrier = pltpu.get_barrier_semaphore()
     for o in range(1, n_emb):
@@ -165,10 +168,14 @@
     n_greet = n_emb - 1
     if fused:
         for o in range(1, n_heads):
-            pl.semaphore_signal(
-                barrier, inc=1, device_id={"heads": head_peer(o)}, device_id_type=MESH
-            )
-        n_greet += n_heads - 1
+            for across in (e, e + 1 - 2 * core):
+                pl.semaphore_signal(
+                    barrier,
+                    inc=1,
+                    device_id={"emb": across, "heads": head_peer(o)},
+                    device_id_type=MESH,
+                )
+        n_greet += 2 * (n_heads - 1)
     elif span > 1:
         for o in range(1, span):
             pl.semaphore_signal(
@@ -179,10 +186,8 @@
             )
         n_greet += span - 1
 
-    made = []
-
-    def send(src, dst, where):
-        at = len(made)
+    def send(name, src, dst, where):
+        at = GROUPS.index(name) if isinstance(name, str) else len(GROUPS) + name
         copy = pltpu.make_async_remote_copy(
             src_ref=src,
             dst_ref=dst,
@@ -192,20 +197,23 @@
             device_id_type=MESH,
         )
         copy.start()
-        made.append(copy)
-        return copy
-
-    def send_emb(src, dst):
-        sent = []
+
+    def send_emb(name, src, dst):
         for o in range(n_emb - 1, 0, -1):
             peer = emb_peer(o)
-            sent.append(send(src.at[peer], dst.at[o - 1], {"emb": peer}))
-        return sent
-
-    def arrived(group_of, name):
-        for copy in group_of:
-            with jax.named_scope(name):
-                copy.wait_recv()
+            send(name, src.at[peer], dst.at[o - 1], {"emb": peer})
+
+    def spread(name, ref):
+        for o in range(n_emb - 1, 0, -1):
+            send(name, ref.at[e], ref.at[e], {"emb": emb_peer(o)})
+
+    def drain(sems, name, like):
+        at = GROUPS.index(name) if isinstance(name, str) else len(GROUPS) + name
+        pltpu.make_async_copy(like, like, sems.at[at]).wait()
+
+    def arrived(name, like):
+        with jax.named_scope("R_" + str(name)):
+            drain(recv_sem, name, like)
 
     heads_at = lax.broadcasted_iota(jnp.int32, (hd, di), 0)
     chans_at = lax.broadcasted_iota(jnp.int32, (hd, di), 1)
@@ -238,33 +246,24 @@
     for peer in range(n_emb):
         dsend[peer, :, 0:hd] = part[peer * bd : (peer + 1) * bd]
 
-    greet_at = min(2, n_chunk)
-    x_copies = []
-    for c in range(n_chunk):
+    greet_at = min(2, n_chunk - 1)
+    for c in range(n_chunk):
+        ready(("x", c))
+        project(wx_v[c], xpart.at[c], xsend.at[c])
         if c == greet_at:
             with jax.named_scope("BARRIER"):
                 pl.semaphore_wait(barrier, n_greet)
-            b_copies = send_emb(bsend, brecv)
-            d_copies = send_emb(dsend, drecv)
+            send_emb("bc", bsend, brecv)
+            send_emb("dt", dsend, drecv)
             for k in range(c):
-                x_copies.append(send_emb(xsend.at[k], xrecv.at[k]))
-        ready(("x", c))
-        project(wx_v[c], xpart.at[c], xsend.at[c])
+                send_emb("x", xsend.at[k], xrecv.at[k])
         if c >= greet_at:
-            x_copies.append(send_emb(xsend.at[c], xrecv.at[c]))
-    if greet_at >= n_chunk:
-        pl.semaphore_wait(barrier, n_greet)
-        b_copies = send_emb(bsend, brecv)
-        d_copies = send_emb(dsend, drecv)
-        for k in range(n_chunk):
-            x_copies.append(send_emb(xsend.at[k], xrecv.at[k]))
-
-    z_copies = []
+            send_emb("x", xsend.at[c], xrecv.at[c])
 
     def do_z(c):
         ready(("z", c))
         project(wz_v[c], zpart.at[c], zsend.at[c])
-        z_copies.append(send_emb(zsend.at[c], zrecv.at[c]))
+        send_emb("z", zsend.at[c], zrecv.at[c])
 
     def total_of(own, got):
         value = own[e]
@@ -280,12 +279,12 @@
     for name in ("dtb", "alog", "skip", "convx", "convwx", "gain"):
         ready(name)
 
-    early = max(n_chunk - 2, 0)
+    early = max(n_chunk - EARLY, 0)
     for c in range(early):
         do_z(c)
 
-    arrived(b_copies, "BRECV")
-    arrived(d_copies, "DRECV")
+    arrived("bc", brecv)
+    arrived("dt", drecv)
     b_all = total_of(bpart, brecv)
     bc = []
     for half in range(2):
@@ -305,26 +304,14 @@
     decay_c = by_chan[bd : 2 * bd]
     skip_c = by_chan[2 * bd : 3 * bd]
 
-    for c in range(early, n_chunk - 1):
+    for c in range(early, n_chunk):
         do_z(c)
-
-    for c in range(n_chunk):
-        arrived(x_copies[c], "XRECV")
-        here = slice(c * chunk, (c + 1) * chunk)
-        x_base = conv_prev(convx_v.at[:, :, here], convwx_ref[:, here])
-        x_all = total_of(xpart.at[c], xrecv.at[c])
-        x_conv = silu(x_base + x_all * convwx_ref[k_prev : k_prev + 1, here])
-        push = step_c[:, here] * x_conv
-        rows = jnp.concatenate([push, decay_c[:, here]], axis=0)
-        cols_v[here, :] = jnp.transpose(rows)
-        xc_v[:, here] = skip_c[:, here] * x_conv + push * b_dot_c
-    do_z(n_chunk - 1)
 
     rows_at = min(256, chunk)
     row = lax.broadcasted_iota(jnp.int32, (2 * bd, chunk), 0)
-    raws = []
 
     def readout(c):
+        ready(("s", c))
         found = None
         for b in range(bd):
             got = lax.dot_general(
@@ -335,9 +322,27 @@
             )
             mine = (row == b) | (row == bd + b)
             found = got if found is None else jnp.where(mine, got, found)
-        raws.append(found[0:bd] + found[bd : 2 * bd])
+        return found[0:bd] + found[bd : 2 * bd]
+
+    raws = [readout(c) for c in range(n_chunk - 1)]
+    arrived("x", xrecv)
+    pushes = []
+    adds = []
+    for c in range(n_chunk):
+        here = slice(c * chunk, (c + 1) * chunk)
+        x_base = conv_prev(convx_v.at[:, :, here], convwx_ref[:, here])
+        x_all = total_of(xpart.at[c], xrecv.at[c])
+        x_conv = silu(x_base + x_all * convwx_ref[k_prev : k_prev + 1, here])
+        push = step_c[:, here] * x_conv
+        pushes.append(push)
+        adds.append(skip_c[:, here] * x_conv + push * b_dot_c)
+    raws.append(readout(n_chunk - 1))
 
     def update(c):
+        here = slice(c * chunk, (c + 1) * chunk)
+        rows = jnp.concatenate([pushes[c], decay_c[:, here]], axis=0)
+        cols_v[here, :] = jnp.transpose(rows)
+
         def step_of(j, carry):
             at = pl.ds(pl.multiple_of(c * chunk + j * rows_at, rows_at), rows_at)
             for b in range(bd):
@@ -349,121 +354,123 @@
         with jax.named_scope("UPD"):
             lax.fori_loop(0, chunk // rows_at, step_of, 0)
 
-    late = n_chunk // 2
-    for c in range(n_chunk):
-        ready(("s", c))
-        readout(c)
-        if c < late:
-            update(c)
-
-    a_copies = []
+    arrived("z", zrecv)
     total = None
     for c in range(n_chunk):
-        arrived(z_copies[c], "ZRECV")
         here = slice(c * chunk, (c + 1) * chunk)
         z_all = total_of(zpart.at[c], zrecv.at[c])
-        read = decay_c[:, here] * raws[c] + xc_v[:, here]
-        gated = read * silu(z_all)
+        gated = (decay_c[:, here] * raws[c] + adds[c]) * silu(z_all)
         squares = jnp.sum(gated * gated, axis=1, keepdims=True)
         total = squares if total is None else total + squares
         ag_v[c, e] = (gated * gain_ref[:, here]).astype(BF16)
-        sent = []
-        for o in range(n_emb - 1, 0, -1):
-            sent.append(send(ag_v.at[c, e], ag_v.at[c, e], {"emb": emb_peer(o)}))
-        a_copies.append(sent)
-    q_copies = []
+        spread(c, ag_v.at[c])
     if span > 1:
         sq_send[...] = jnp.broadcast_to(total, (bd, LANES))
         for o in range(1, span):
-            q_copies.append(
-                send(
-                    sq_send,
-                    sq_recv.at[o - 1],
-                    {"heads": group * span + lax.rem(h % span + o, span)},
-                )
-            )
-        for o, copy in enumerate(q_copies):
-            copy.wait_recv()
+            peer = group * span + lax.rem(h % span + o, span)
+            send("sq", sq_send, sq_recv.at[o - 1], {"heads": peer})
+        arrived("sq", sq_recv)
+        for o in range(span - 1):
             total = total + sq_recv[o][:, 0:1]
     ss_v[e] = jnp.broadcast_to(total, (bd, LANES))
-    s_copies = []
-    for o in range(n_emb - 1, 0, -1):
-        s_copies.append(send(ss_v.at[e], ss_v.at[e], {"emb": emb_peer(o)}))
-
-    for c in range(late, n_chunk):
+    spread("ss", ss_v)
+
+    late = n_chunk // 2
+    for c in range(late):
         update(c)
 
     acc = None
     for c in range(n_chunk):
-        arrived(a_copies[c], "ARECV")
+        arrived(c, ag_v.at[c, 0:e_n])
         whole = jnp.concatenate([ag_v[c, i].astype(F32) for i in range(n_emb)], axis=0).astype(BF16)
         ready(("o", c))
         part = jnp.dot(whole, wout_v[c], preferred_element_type=F32)
         acc = part if acc is None else acc + part
-    arrived(s_copies, "SRECV")
+    arrived("ss", ss_v.at[0:e_n])
     sums = jnp.concatenate([ss_v[i] for i in range(n_emb)], axis=0)[:, 0:1]
     inv_rms = lax.rsqrt(sums / (H * P_SIZE // G) + 1e-05)
     acc = acc * inv_rms
     if not fused:
         out_ref[...] = acc
+        for c in range(late, n_chunk):
+            update(c)
     else:
-        acc_v[...] = acc
-        last = []
-        for i in range(n_heads - 1):
-            peer = head_peer(n_heads - 1 - i)
-            at = pl.ds(pl.multiple_of(peer * ochunk, ochunk), ochunk)
-            rs_send[i] = acc_v[:, at].astype(BF16)
-            last.append(send(rs_send.at[i], rs_recv.at[i], {"heads": peer}))
-        own = acc_v[:, pl.ds(pl.multiple_of(h * ochunk, ochunk), ochunk)]
-        for i, copy in enumerate(last):
-            with jax.named_scope("RRECV"):
-                copy.wait_recv()
-            own = own + rs_recv[i].astype(F32)
-        fin_send[...] = own.astype(BF16)
-        f_copies = []
-        for o in range(n_heads - 1, 0, -1):
-            f_copies.append(send(fin_send, fin_v.at[h], {"heads": head_peer(o)}))
-        out_ref[h] = fin_send[...]
-        for i, copy in enumerate(f_copies):
-            with jax.named_scope("FRECV"):
-                copy.wait_recv()
-        for i in range(1, n_heads):
-            peer = head_peer(i)
-            out_ref[peer] = fin_v[peer]
+        ochunk = cols // n_own
+        for j in range(n_own):
+            rs_send[j] = acc[:, j * ochunk : (j + 1) * ochunk].astype(BF16)
+        far = (n_own // 2) * (1 - h // (n_heads // 2))
+        for i in range(n_own):
+            j = lax.rem(i + far, n_own)
+
+            @pl.when((core == 0) | (h != first_own + j))
+            def _():
+                send(
+                    "rs",
+                    rs_send.at[j],
+                    rs_recv.at[core * n_heads + h],
+                    {"emb": e + 1 - core, "heads": first_own + j},
+                )
+
+        for c in range(late, n_chunk):
+            update(c)
+
+        @pl.when(owner)
+        def _():
+            mine = h - first_own
+            rs_recv[n_heads + h] = rs_send[mine]
+            arrived("rs", rs_recv.at[0 : 2 * n_heads - 1])
+            for k in range(2):
+                whole_sum = rs_recv[k * n_heads].astype(F32)
+                for i in range(1, n_heads):
+                    whole_sum = whole_sum + rs_recv[k * n_heads + i].astype(F32)
+                fin_send[k] = whole_sum.astype(BF16)
+            for o in range(n_heads - 1, -1, -1):
+                peer = head_peer(o)
+                send("ag", fin_send.at[0], out_ref.at[mine], {"emb": e - 1, "heads": peer})
+                if o > 0:
+                    send("ag", fin_send.at[1], out_ref.at[mine], {"heads": peer})
+            out_ref[mine] = fin_send[1]
+            arrived("ag", out_ref.at[0 : n_own - 1])
+            drain(send_sem, "ag", rs_recv.at[0 : 2 * n_heads - 1])
+            drain(send_sem, "rs", rs_send.at[0 : n_own - 1])
+
+        @pl.when(jnp.logical_not(owner))
+        def _():
+            arrived("ag", out_ref)
+            drain(send_sem, "rs", rs_send)
+
     with jax.named_scope("SENT"):
-        for copy in made:
-            copy.wait_send()
-
-
-def write_kernel(n_parts, n_heads, ochunk, has_out, *refs):
+        drain(send_sem, "bc", brecv)
+        drain(send_sem, "dt", drecv)
+        drain(send_sem, "x", xrecv)
+        drain(send_sem, "z", zrecv)
+        for c in range(n_chunk):
+            drain(send_sem, c, ag_v.at[c, 0:e_n])
+        drain(send_sem, "ss", ss_v.at[0:e_n])
+        if span > 1:
+            drain(send_sem, "sq", sq_recv)
+
+
+def write_kernel(n_parts, n_own, has_out, *refs):
     if has_out:
         st_v, fin_v, st_hbm, out_hbm, sem = refs
     else:
         st_v, st_hbm, sem = refs
-    made = []
     if has_out:
-        for i in range(n_heads):
-            made.append(
-                pltpu.make_async_copy(
-                    fin_v.at[i],
-                    out_hbm.at[:, i * ochunk : (i + 1) * ochunk],
-                    sem.at[i],
-                )
-            )
-            made[-1].start()
+        ochunk = fin_v.shape[2]
+        for i in range(n_own):
+            pltpu.make_async_copy(
+                fin_v.at[i], out_hbm.at[:, i * ochunk : (i + 1) * ochunk], sem.at[1]
+            ).start()
     bd, di, _ = st_v.shape
     rows = di // n_parts
     for b in range(bd):
         for i in range(n_parts):
             part = pl.ds(i * rows, rows)
-            made.append(
-                pltpu.make_async_copy(
-                    st_v.at[b, part], st_hbm.at[b, part], sem.at[n_heads + b * n_parts + i]
-                )
-            )
-            made[-1].start()
-    for copy in made:
-        copy.wait()
+            pltpu.make_async_copy(st_v.at[b, part], st_hbm.at[b, part], sem.at[0]).start()
+    if has_out:
+        pltpu.make_async_copy(fin_v, fin_v, sem.at[1]).wait()
+    pltpu.make_async_copy(st_v, st_hbm, sem.at[0]).wait()
 
 
 def in_hbm(*arrays):
@@ -496,22 +503,21 @@
     di = w_x.shape[1]
     hd = w_dt.shape[1]
     cols = w_out.shape[1]
-    fused = cols % (n_heads * LANES) == 0
+    n_own = n_heads // 2
+    fused = n_heads % 4 == 0 and n_emb % 2 == 0 and cols % (n_heads * LANES) == 0
     chunk = min(512, di)
-    ochunk = cols // n_heads if fused else cols
-    dims = (n_emb, n_heads, batch, bd, di, hd, cols, chunk, ochunk, fused, span)
+    dims = (n_emb, n_heads, batch, bd, di, hd, cols, chunk, n_own, fused, span)
     n_chunk = di // chunk
-    n_streams = 14 + 4 * n_chunk
     vm = pl.BlockSpec(memory_space=pltpu.VMEM)
     hbm = pl.BlockSpec(memory_space=pltpu.HBM)
     dma = pltpu.SemaphoreType.DMA
-    rs_n = max(n_heads - 1, 1) if fused else 1
-    rs_shape = (batch, ochunk) if fused else (batch, LANES)
-    fin_n = n_heads if fused else 1
+    ochunk = cols // n_own if fused else LANES
+    own_n = n_own if fused else 1
+    all_n = 2 * n_heads if fused else 1
     e_n = max(n_emb - 1, 1)
     q_n = max(span - 1, 1)
-    n_remote = (3 + 3 * n_chunk) * e_n + q_n + 2 * rs_n
-    out_shape = (n_heads, batch, ochunk) if fused else (batch, cols)
+    n_remote = len(GROUPS) + n_chunk
+    out_shape = (n_own, batch, ochunk) if fused else (batch, cols)
     out, new_state = pl.pallas_call(
         functools.partial(kernel, dims),
         out_shape=(
@@ -547,17 +553,14 @@
             pltpu.VMEM((n_chunk, n_emb, bd, chunk), BF16),
             pltpu.VMEM((n_chunk, e_n, bd, chunk), BF16),
             pltpu.VMEM((di, 2 * bd), F32),
-            pltpu.VMEM((bd, di), F32),
             pltpu.VMEM((n_chunk, n_emb, bd, chunk), BF16),
             pltpu.VMEM((n_emb, bd, LANES), F32),
-            pltpu.VMEM((batch, cols), F32),
-            pltpu.VMEM((rs_n,) + rs_shape, BF16),
-            pltpu.VMEM((rs_n,) + rs_shape, BF16),
-            pltpu.VMEM(rs_shape, BF16),
-            pltpu.VMEM((fin_n,) + rs_shape, BF16),
+            pltpu.VMEM((own_n, batch, ochunk), BF16),
+            pltpu.VMEM((all_n, batch, ochunk), BF16),
+            pltpu.VMEM((2, batch, ochunk), BF16),
             pltpu.VMEM((bd, LANES), F32),
             pltpu.VMEM((q_n, bd, LANES), F32),
-            dma((n_streams,)),
+            dma((DEPTH,)),
             dma((n_remote,)),
             dma((n_remote,)),
         ],
@@ -585,9 +588,9 @@
     )
     n_parts = max(di // 512, 1)
     params = pltpu.CompilerParams(vmem_limit_bytes=2 * 1024 * 1024)
-    sems = dma((n_heads + bd * n_parts,))
+    sems = dma((2,))
     state_shape = jax.ShapeDtypeStruct((bd, di, N), F32)
-    write = functools.partial(write_kernel, n_parts, n_heads, ochunk, fused)
+    write = functools.partial(write_kernel, n_parts, n_own, fused)
     if fused:
         new_state, mixed = pl.pallas_call(
             write,

time: 32 us -> 29.7 us (0.928)
  Pallas kernels: 31.2 us -> 28.9 us
    pallas_call x1, Pallas kernels: 27.7 us -> 25.5 us  [on_device(): pl.pallas_call(functools.partial(kernel, dims), out_shape=(pltpu.VMEM(out...]
where the time goes in v2:
time: 29.7 us; the launch traced here: 29.5 us
  Pallas kernels  28.9 us (97%)
  between operations  0.64 us (2%)
    pallas_call x1, Pallas kernels, on_device(): pl.pallas_call(functools.partial(kernel, dims), out_shape=(pltpu.VMEM(out...  25.5 us
    pallas_call x1, Pallas kernels, on_device(): pl.pallas_call(write, out_shape=(state_shape, jax.ShapeDtypeStruct((batch...  3.31 us

profile of v2, /device:TPU:0, one launch (start us, length us, event | category | flops | bytes accessed | tf_op | source)
XLA Modules:
  0.0 29.5 jit_solution(7767095751722712818)
XLA Ops:
  0.6 25.5 %shard_map.158 = (bf16[4,16,512]{2,1,0:T(8,128)(2,1)S(1)}, f32[4,2048,256]{2,1,0:T(8,128)S(1)}) custom-call(bf16[16,2048]{1,0:T(8,128)(2,1)} %hidden_hbm.1, f32[1,32]{1,0:T(1,128)} %bitcast.14, f32[1,32]{1,0:T(1,128)} %bitcast.15, f32[1,32]{1,0:T(1,128)} %bitcast.16, bf16[3,4,2048]{2,1,0:T(4,128)(2,1)} %bitcast.12, f32[4,2048]{1,0:T(4,128)} %convwx_hbm.1, ...), custom_call_target="tpu_custom_call" | custom-call | tf_op jit(solution)/shard_map/pallas_call | solution.py:521
  26.2 3.3 %shard_map.159 = (f32[4,2048,256]{2,1,0:T(8,128)}, bf16[16,2048]{1,0:T(8,128)(2,1)}) custom-call(f32[4,2048,256]{2,1,0:T(8,128)S(1)} %get-tuple-element.6.refs_0_, bf16[4,16,512]{2,1,0:T(8,128)(2,1)S(1)} %get-tuple-element.7.refs_1_), custom_call_target="tpu_custom_call" | custom-call | tf_op jit(solution)/shard_map/pallas_call | solution.py:595

commit v3 on v2

--- a/solution.py
+++ b/solution.py
@@ -13,8 +13,7 @@
 G = 8
 LANES = 128
 DEPTH = 18
-EARLY = 1
-GROUPS = ("bc", "dt", "x", "z", "ss", "sq", "rs", "ag")
+GROUPS = ("bc", "dt", "x", "ss", "sq", "rs", "ag")
 MESH = pl.DeviceIdType.MESH
 F32 = jnp.float32
 BF16 = jnp.bfloat16
@@ -130,6 +129,8 @@
     stream("dt", wdt_hbm, wdt_v)
     for c in range(n_chunk):
         stream(("x", c), wx_hbm.at[:, pl.ds(c * chunk, chunk)], wx_v.at[c])
+    for c in range(n_chunk):
+        stream(("z", c), wz_hbm.at[:, pl.ds(c * chunk, chunk)], wz_v.at[c])
     for half in range(2):
         off = pl.multiple_of(half * G * N + group * N, N)
         stream(("cb", half), convbc_hbm.at[:, :, pl.ds(off, N)], convbc_v.at[half])
@@ -140,8 +141,6 @@
     stream("convx", convx_hbm, convx_v)
     stream("convwx", convwx_hbm, convwx_ref)
     stream("gain", gain_hbm, gain_ref)
-    for c in range(n_chunk):
-        stream(("z", c), wz_hbm.at[:, pl.ds(c * chunk, chunk)], wz_v.at[c])
     for c in range(n_chunk):
         part = pl.ds(c * chunk, chunk)
         stream(("s", c), state_hbm.at[:, part], st_ref.at[:, part])
@@ -186,8 +185,14 @@
             )
         n_greet += span - 1
 
+    def place(name):
+        if name in GROUPS:
+            return GROUPS.index(name)
+        kind, c = name
+        return len(GROUPS) + 2 * c + (kind == "z")
+
     def send(name, src, dst, where):
-        at = GROUPS.index(name) if isinstance(name, str) else len(GROUPS) + name
+        at = place(name)
         copy = pltpu.make_async_remote_copy(
             src_ref=src,
             dst_ref=dst,
@@ -208,11 +213,11 @@
             send(name, ref.at[e], ref.at[e], {"emb": emb_peer(o)})
 
     def drain(sems, name, like):
-        at = GROUPS.index(name) if isinstance(name, str) else len(GROUPS) + name
+        at = place(name)
         pltpu.make_async_copy(like, like, sems.at[at]).wait()
 
     def arrived(name, like):
-        with jax.named_scope("R_" + str(name)):
+        with jax.named_scope("R_" + (name if name in GROUPS else name[0] + str(name[1]))):
             drain(recv_sem, name, like)
 
     heads_at = lax.broadcasted_iota(jnp.int32, (hd, di), 0)
@@ -263,13 +268,16 @@
     def do_z(c):
         ready(("z", c))
         project(wz_v[c], zpart.at[c], zsend.at[c])
-        send_emb("z", zsend.at[c], zrecv.at[c])
+        send_emb(("z", c), zsend.at[c], zrecv.at[c])
 
     def total_of(own, got):
         value = own[e]
         for o in range(n_emb - 1):
             value = value + got[o].astype(F32)
         return value
+
+    for c in range(n_chunk):
+        do_z(c)
 
     bc_base = []
     for half in range(2):
@@ -278,10 +286,6 @@
         bc_base.append(conv_prev(convbc_v.at[half], convwbc_v[half]))
     for name in ("dtb", "alog", "skip", "convx", "convwx", "gain"):
         ready(name)
-
-    early = max(n_chunk - EARLY, 0)
-    for c in range(early):
-        do_z(c)
 
     arrived("bc", brecv)
     arrived("dt", drecv)
@@ -304,9 +308,6 @@
     decay_c = by_chan[bd : 2 * bd]
     skip_c = by_chan[2 * bd : 3 * bd]
 
-    for c in range(early, n_chunk):
-        do_z(c)
-
     rows_at = min(256, chunk)
     row = lax.broadcasted_iota(jnp.int32, (2 * bd, chunk), 0)
 
@@ -324,7 +325,6 @@
             found = got if found is None else jnp.where(mine, got, found)
         return found[0:bd] + found[bd : 2 * bd]
 
-    raws = [readout(c) for c in range(n_chunk - 1)]
     arrived("x", xrecv)
     pushes = []
     adds = []
@@ -336,7 +336,6 @@
         push = step_c[:, here] * x_conv
         pushes.append(push)
         adds.append(skip_c[:, here] * x_conv + push * b_dot_c)
-    raws.append(readout(n_chunk - 1))
 
     def update(c):
         here = slice(c * chunk, (c + 1) * chunk)
@@ -354,16 +353,17 @@
         with jax.named_scope("UPD"):
             lax.fori_loop(0, chunk // rows_at, step_of, 0)
 
-    arrived("z", zrecv)
     total = None
     for c in range(n_chunk):
         here = slice(c * chunk, (c + 1) * chunk)
+        raw = readout(c)
+        arrived(("z", c), zrecv.at[c])
         z_all = total_of(zpart.at[c], zrecv.at[c])
-        gated = (decay_c[:, here] * raws[c] + adds[c]) * silu(z_all)
+        gated = (decay_c[:, here] * raw + adds[c]) * silu(z_all)
+        ag_v[c, e] = (gated * gain_ref[:, here]).astype(BF16)
+        spread(("a", c), ag_v.at[c])
         squares = jnp.sum(gated * gated, axis=1, keepdims=True)
         total = squares if total is None else total + squares
-        ag_v[c, e] = (gated * gain_ref[:, here]).astype(BF16)
-        spread(c, ag_v.at[c])
     if span > 1:
         sq_send[...] = jnp.broadcast_to(total, (bd, LANES))
         for o in range(1, span):
@@ -375,13 +375,13 @@
     ss_v[e] = jnp.broadcast_to(total, (bd, LANES))
     spread("ss", ss_v)
 
-    late = n_chunk // 2
+    late = n_chunk // 4
     for c in range(late):
         update(c)
 
     acc = None
     for c in range(n_chunk):
-        arrived(c, ag_v.at[c, 0:e_n])
+        arrived(("a", c), ag_v.at[c, 0:e_n])
         whole = jnp.concatenate([ag_v[c, i].astype(F32) for i in range(n_emb)], axis=0).astype(BF16)
         ready(("o", c))
         part = jnp.dot(whole, wout_v[c], preferred_element_type=F32)
@@ -443,9 +443,9 @@
         drain(send_sem, "bc", brecv)
         drain(send_sem, "dt", drecv)
         drain(send_sem, "x", xrecv)
-        drain(send_sem, "z", zrecv)
         for c in range(n_chunk):
-            drain(send_sem, c, ag_v.at[c, 0:e_n])
+            drain(send_sem, ("z", c), zrecv.at[c])
+            drain(send_sem, ("a", c), ag_v.at[c, 0:e_n])
         drain(send_sem, "ss", ss_v.at[0:e_n])
         if span > 1:
             drain(send_sem, "sq", sq_recv)
@@ -516,7 +516,7 @@
     all_n = 2 * n_heads if fused else 1
     e_n = max(n_emb - 1, 1)
     q_n = max(span - 1, 1)
-    n_remote = len(GROUPS) + n_chunk
+    n_remote = len(GROUPS) + 2 * n_chunk
     out_shape = (n_own, batch, ochunk) if fused else (batch, cols)
     out, new_state = pl.pallas_call(
         functools.partial(kernel, dims),

time: 29.7 us -> 28.5 us (0.960)
  Pallas kernels: 28.9 us -> 27.7 us
    pallas_call x1, Pallas kernels: 25.5 us -> 24.4 us  [on_device(): pl.pallas_call(functools.partial(kernel, dims), out_shape=(pltpu.VMEM(out...]
where the time goes in v3:
time: 28.5 us; the launch traced here: 28.4 us
  Pallas kernels  27.7 us (97%)
  between operations  0.64 us (2%)
    pallas_call x1, Pallas kernels, on_device(): pl.pallas_call(functools.partial(kernel, dims), out_shape=(pltpu.VMEM(out...  24.4 us
    pallas_call x1, Pallas kernels, on_device(): pl.pallas_call(write, out_shape=(state_shape, jax.ShapeDtypeStruct((batch...  3.31 us

profile of v3, /device:TPU:0, one launch (start us, length us, event | category | flops | bytes accessed | tf_op | source)
XLA Modules:
  0.0 28.4 jit_solution(5895893914841486682)
XLA Ops:
  0.6 24.4 %shard_map.158 = (bf16[4,16,512]{2,1,0:T(8,128)(2,1)S(1)}, f32[4,2048,256]{2,1,0:T(8,128)S(1)}) custom-call(bf16[16,2048]{1,0:T(8,128)(2,1)} %hidden_hbm.1, f32[1,32]{1,0:T(1,128)} %bitcast.14, f32[1,32]{1,0:T(1,128)} %bitcast.15, f32[1,32]{1,0:T(1,128)} %bitcast.16, bf16[3,4,2048]{2,1,0:T(4,128)(2,1)} %bitcast.12, f32[4,2048]{1,0:T(4,128)} %convwx_hbm.1, ...), custom_call_target="tpu_custom_call" | custom-call | tf_op jit(solution)/shard_map/pallas_call | solution.py:521
  25.1 3.3 %shard_map.159 = (f32[4,2048,256]{2,1,0:T(8,128)}, bf16[16,2048]{1,0:T(8,128)(2,1)}) custom-call(f32[4,2048,256]{2,1,0:T(8,128)S(1)} %get-tuple-element.6.refs_0_, bf16[4,16,512]{2,1,0:T(8,128)(2,1)S(1)} %get-tuple-element.7.refs_1_), custom_call_target="tpu_custom_call" | custom-call | tf_op jit(solution)/shard_map/pallas_call | solution.py:595

commit v4 on v3

--- a/solution.py
+++ b/solution.py
@@ -13,7 +13,7 @@
 G = 8
 LANES = 128
 DEPTH = 18
-GROUPS = ("bc", "dt", "x", "ss", "sq", "rs", "ag")
+GROUPS = ("bc", "dt", "x", "ss", "sq", "rs", "ag", "z", "a")
 MESH = pl.DeviceIdType.MESH
 F32 = jnp.float32
 BF16 = jnp.bfloat16
@@ -33,6 +33,14 @@
     mid = rest.astype(BF16)
     low = (rest - mid.astype(F32)).astype(BF16)
     return high, mid, low
+
+
+def pieces_of(n_chunk, chunk):
+    found = [(c, 0, chunk) for c in range(n_chunk)]
+    half = chunk // 2
+    if half % (2 * LANES) == 0:
+        found[-1:] = [(n_chunk - 1, 0, half), (n_chunk - 1, half, half)]
+    return tuple(found)
 
 
 def kernel(
@@ -91,16 +99,14 @@
     send_sem,
     recv_sem,
 ):
-    (n_emb, n_heads, batch, bd, di, hd, cols, chunk, n_own, fused, span) = dims
+    (n_emb, n_heads, batch, bd, di, hd, cols, chunk, pieces, n_own, fused, span) = dims
     e = lax.axis_index("emb")
     h = lax.axis_index("heads")
     group = h // span
     n_chunk = di // chunk
     e_n = n_emb - 1
     core = lax.rem(e, 2)
-    first_own = n_heads // 4
-    in_middle = (h >= first_own) & (h < first_own + n_own)
-    owner = (core == 1) & in_middle
+    partner = e + 1 - 2 * core
 
     def emb_peer(o):
         return lax.rem(e + o, n_emb)
@@ -131,21 +137,21 @@
         stream(("x", c), wx_hbm.at[:, pl.ds(c * chunk, chunk)], wx_v.at[c])
     for c in range(n_chunk):
         stream(("z", c), wz_hbm.at[:, pl.ds(c * chunk, chunk)], wz_v.at[c])
-    for half in range(2):
-        off = pl.multiple_of(half * G * N + group * N, N)
-        stream(("cb", half), convbc_hbm.at[:, :, pl.ds(off, N)], convbc_v.at[half])
-        stream(("cw", half), convwbc_hbm.at[:, pl.ds(off, N)], convwbc_v.at[half])
+    stream("cb", convbc_hbm, convbc_v)
+    stream("cw", convwbc_hbm, convwbc_v)
     stream("dtb", dtb_hbm, dtb_ref)
     stream("alog", alog_hbm, alog_ref)
     stream("skip", skip_hbm, skip_ref)
     stream("convx", convx_hbm, convx_v)
     stream("convwx", convwx_hbm, convwx_ref)
     stream("gain", gain_hbm, gain_ref)
-    for c in range(n_chunk):
-        part = pl.ds(c * chunk, chunk)
-        stream(("s", c), state_hbm.at[:, part], st_ref.at[:, part])
-    for c in range(n_chunk):
-        stream(("o", c), wout_hbm.at[pl.ds(c * chunk, chunk)], wout_v.at[c])
+    for p, (c, lo, width) in enumerate(pieces):
+        part = pl.ds(c * chunk + lo, width)
+        stream(("s", p), state_hbm.at[:, part], st_ref.at[:, part])
+    for p, (c, lo, width) in enumerate(pieces):
+        part = pl.ds(c * chunk + lo, width)
+        stream(("o", p), wout_hbm.at[part], wout_v.at[part])
+
     def advance(slot):
         if queue:
             name, src, dst = queue.pop(0)
@@ -167,7 +173,7 @@
     n_greet = n_emb - 1
     if fused:
         for o in range(1, n_heads):
-            for across in (e, e + 1 - 2 * core):
+            for across in (e, partner):
                 pl.semaphore_signal(
                     barrier,
                     inc=1,
@@ -185,40 +191,39 @@
             )
         n_greet += span - 1
 
-    def place(name):
-        if name in GROUPS:
+    def sent_at(name):
+        return GROUPS.index(name if isinstance(name, str) else name[0])
+
+    def got_at(name):
+        if isinstance(name, str):
             return GROUPS.index(name)
-        kind, c = name
-        return len(GROUPS) + 2 * c + (kind == "z")
+        return len(GROUPS) - 2 + 2 * name[1] + (name[0] == "z")
 
     def send(name, src, dst, where):
-        at = place(name)
-        copy = pltpu.make_async_remote_copy(
+        pltpu.make_async_remote_copy(
             src_ref=src,
             dst_ref=dst,
-            send_sem=send_sem.at[at],
-            recv_sem=recv_sem.at[at],
+            send_sem=send_sem.at[sent_at(name)],
+            recv_sem=recv_sem.at[got_at(name)],
             device_id=where,
             device_id_type=MESH,
-        )
-        copy.start()
+        ).start()
 
     def send_emb(name, src, dst):
         for o in range(n_emb - 1, 0, -1):
             peer = emb_peer(o)
-            send(name, src.at[peer], dst.at[o - 1], {"emb": peer})
+            send(name, src(peer), dst(o - 1), {"emb": peer})
 
     def spread(name, ref):
         for o in range(n_emb - 1, 0, -1):
-            send(name, ref.at[e], ref.at[e], {"emb": emb_peer(o)})
-
-    def drain(sems, name, like):
-        at = place(name)
-        pltpu.make_async_copy(like, like, sems.at[at]).wait()
+            send(name, ref, ref, {"emb": emb_peer(o)})
+
+    def drain(name, like):
+        pltpu.make_async_copy(like, like, send_sem.at[sent_at(name)]).wait()
 
     def arrived(name, like):
-        with jax.named_scope("R_" + (name if name in GROUPS else name[0] + str(name[1]))):
-            drain(recv_sem, name, like)
+        with jax.named_scope("R_" + (name if isinstance(name, str) else name[0] + str(name[1]))):
+            pltpu.make_async_copy(like, like, recv_sem.at[got_at(name)]).wait()
 
     heads_at = lax.broadcasted_iota(jnp.int32, (hd, di), 0)
     chans_at = lax.broadcasted_iota(jnp.int32, (hd, di), 1)
@@ -258,17 +263,15 @@
         if c == greet_at:
             with jax.named_scope("BARRIER"):
                 pl.semaphore_wait(barrier, n_greet)
-            send_emb("bc", bsend, brecv)
-            send_emb("dt", dsend, drecv)
-            for k in range(c):
-                send_emb("x", xsend.at[k], xrecv.at[k])
-        if c >= greet_at:
-            send_emb("x", xsend.at[c], xrecv.at[c])
+            send_emb("bc", lambda peer: bsend.at[peer], lambda o: brecv.at[o])
+            send_emb("dt", lambda peer: dsend.at[peer], lambda o: drecv.at[o])
+        for k in range(0 if c == greet_at else c, c + 1 if c >= greet_at else 0):
+            send_emb("x", lambda peer, k=k: xsend.at[k, peer], lambda o, k=k: xrecv.at[k, o])
 
     def do_z(c):
         ready(("z", c))
         project(wz_v[c], zpart.at[c], zsend.at[c])
-        send_emb(("z", c), zsend.at[c], zrecv.at[c])
+        send_emb(("z", c), lambda peer: zsend.at[c, peer], lambda o: zrecv.at[c, o])
 
     def total_of(own, got):
         value = own[e]
@@ -279,11 +282,12 @@
     for c in range(n_chunk):
         do_z(c)
 
-    bc_base = []
-    for half in range(2):
-        ready(("cb", half))
-        ready(("cw", half))
-        bc_base.append(conv_prev(convbc_v.at[half], convwbc_v[half]))
+    ready("cb")
+    ready("cw")
+    bc_at = [pl.ds(pl.multiple_of(half * G * N + group * N, N), N) for half in range(2)]
+    bc_base = [
+        conv_prev(convbc_v.at[:, :, bc_at[half]], convwbc_v[:, bc_at[half]]) for half in range(2)
+    ]
     for name in ("dtb", "alog", "skip", "convx", "convwx", "gain"):
         ready(name)
 
@@ -293,7 +297,7 @@
     bc = []
     for half in range(2):
         pre = b_all[:, half * N : (half + 1) * N]
-        bc.append(silu(bc_base[half] + pre * convwbc_v[half, k_prev : k_prev + 1, :]))
+        bc.append(silu(bc_base[half] + pre * convwbc_v[k_prev : k_prev + 1, bc_at[half]]))
     b_group, c_group = bc
     c_high, c_low, _ = split3(c_group)
     c_both = jnp.concatenate([c_high.astype(F32), c_low.astype(F32)], axis=0).astype(BF16)
@@ -309,15 +313,17 @@
     skip_c = by_chan[2 * bd : 3 * bd]
 
     rows_at = min(256, chunk)
-    row = lax.broadcasted_iota(jnp.int32, (2 * bd, chunk), 0)
-
-    def readout(c):
-        ready(("s", c))
+
+    def readout(p):
+        c, lo, width = pieces[p]
+        part = pl.ds(c * chunk + lo, width)
+        row = lax.broadcasted_iota(jnp.int32, (2 * bd, width), 0)
+        ready(("s", p))
         found = None
         for b in range(bd):
             got = lax.dot_general(
                 c_both,
-                st_ref[b, c * chunk : (c + 1) * chunk, :].astype(BF16),
+                st_ref[b, part, :].astype(BF16),
                 (((1,), (1,)), ((), ())),
                 preferred_element_type=F32,
             )
@@ -354,40 +360,51 @@
             lax.fori_loop(0, chunk // rows_at, step_of, 0)
 
     total = None
-    for c in range(n_chunk):
-        here = slice(c * chunk, (c + 1) * chunk)
-        raw = readout(c)
-        arrived(("z", c), zrecv.at[c])
-        z_all = total_of(zpart.at[c], zrecv.at[c])
-        gated = (decay_c[:, here] * raw + adds[c]) * silu(z_all)
-        ag_v[c, e] = (gated * gain_ref[:, here]).astype(BF16)
-        spread(("a", c), ag_v.at[c])
-        squares = jnp.sum(gated * gated, axis=1, keepdims=True)
-        total = squares if total is None else total + squares
+    for p, (c, lo, width) in enumerate(pieces):
+        here = slice(lo, lo + width)
+        at = slice(c * chunk + lo, c * chunk + lo + width)
+        raw = readout(p)
+        if lo == 0:
+            arrived(("z", c), zrecv.at[c])
+        z_all = zpart[c, e, :, here]
+        for o in range(e_n):
+            z_all = z_all + zrecv[c, o, :, here].astype(F32)
+        gated = (decay_c[:, at] * raw + adds[c][:, here]) * silu(z_all)
+        ag_v[c, e, :, here] = (gated * gain_ref[:, at]).astype(BF16)
+        spread(("a", p), ag_v.at[c, e, :, here])
+        for lane in range(0, width, LANES):
+            squares = gated[:, lane : lane + LANES]
+            squares = squares * squares
+            total = squares if total is None else total + squares
     if span > 1:
-        sq_send[...] = jnp.broadcast_to(total, (bd, LANES))
+        sq_send[...] = total
         for o in range(1, span):
             peer = group * span + lax.rem(h % span + o, span)
             send("sq", sq_send, sq_recv.at[o - 1], {"heads": peer})
         arrived("sq", sq_recv)
         for o in range(span - 1):
-            total = total + sq_recv[o][:, 0:1]
-    ss_v[e] = jnp.broadcast_to(total, (bd, LANES))
-    spread("ss", ss_v)
+            total = total + sq_recv[o]
+    ss_v[e] = total
+    spread("ss", ss_v.at[e])
 
     late = n_chunk // 4
     for c in range(late):
         update(c)
 
     acc = None
-    for c in range(n_chunk):
-        arrived(("a", c), ag_v.at[c, 0:e_n])
-        whole = jnp.concatenate([ag_v[c, i].astype(F32) for i in range(n_emb)], axis=0).astype(BF16)
-        ready(("o", c))
-        part = jnp.dot(whole, wout_v[c], preferred_element_type=F32)
+    for p, (c, lo, width) in enumerate(pieces):
+        here = slice(lo, lo + width)
+        arrived(("a", p), ag_v.at[c, 0:e_n, :, here])
+        whole = jnp.concatenate(
+            [ag_v[c, i, :, here].astype(F32) for i in range(n_emb)], axis=0
+        ).astype(BF16)
+        ready(("o", p))
+        weights = wout_v[c * chunk + lo : c * chunk + lo + width]
+        part = jnp.dot(whole, weights, preferred_element_type=F32)
         acc = part if acc is None else acc + part
     arrived("ss", ss_v.at[0:e_n])
-    sums = jnp.concatenate([ss_v[i] for i in range(n_emb)], axis=0)[:, 0:1]
+    sums = jnp.concatenate([ss_v[i] for i in range(n_emb)], axis=0)
+    sums = jnp.sum(sums, axis=1, keepdims=True)
     inv_rms = lax.rsqrt(sums / (H * P_SIZE // G) + 1e-05)
     acc = acc * inv_rms
     if not fused:
@@ -398,57 +415,35 @@
         ochunk = cols // n_own
         for j in range(n_own):
             rs_send[j] = acc[:, j * ochunk : (j + 1) * ochunk].astype(BF16)
-        far = (n_own // 2) * (1 - h // (n_heads // 2))
-        for i in range(n_own):
-            j = lax.rem(i + far, n_own)
-
-            @pl.when((core == 0) | (h != first_own + j))
-            def _():
-                send(
-                    "rs",
-                    rs_send.at[j],
-                    rs_recv.at[core * n_heads + h],
-                    {"emb": e + 1 - core, "heads": first_own + j},
-                )
-
-        for c in range(late, n_chunk):
+        for m in range(n_own - 1, -1, -1):
+            peer = head_peer(m)
+            send("rs", rs_send.at[peer], rs_recv.at[m], {"emb": partner, "heads": peer})
+
+        for c in range(late, 2 * late):
             update(c)
 
-        @pl.when(owner)
-        def _():
-            mine = h - first_own
-            rs_recv[n_heads + h] = rs_send[mine]
-            arrived("rs", rs_recv.at[0 : 2 * n_heads - 1])
-            for k in range(2):
-                whole_sum = rs_recv[k * n_heads].astype(F32)
-                for i in range(1, n_heads):
-                    whole_sum = whole_sum + rs_recv[k * n_heads + i].astype(F32)
-                fin_send[k] = whole_sum.astype(BF16)
-            for o in range(n_heads - 1, -1, -1):
-                peer = head_peer(o)
-                send("ag", fin_send.at[0], out_ref.at[mine], {"emb": e - 1, "heads": peer})
-                if o > 0:
-                    send("ag", fin_send.at[1], out_ref.at[mine], {"heads": peer})
-            out_ref[mine] = fin_send[1]
-            arrived("ag", out_ref.at[0 : n_own - 1])
-            drain(send_sem, "ag", rs_recv.at[0 : 2 * n_heads - 1])
-            drain(send_sem, "rs", rs_send.at[0 : n_own - 1])
-
-        @pl.when(jnp.logical_not(owner))
-        def _():
-            arrived("ag", out_ref)
-            drain(send_sem, "rs", rs_send)
+        arrived("rs", rs_recv)
+        whole_sum = rs_recv[0].astype(F32)
+        for m in range(1, n_own):
+            whole_sum = whole_sum + rs_recv[m].astype(F32)
+        fin_send[...] = whole_sum.astype(BF16)
+        for peer in range(n_own):
+            send("ag", fin_send, out_ref.at[h], {"emb": partner, "heads": peer})
+        for c in range(2 * late, n_chunk):
+            update(c)
+        arrived("ag", out_ref)
+        drain("rs", rs_send)
+        drain("ag", rs_recv)
 
     with jax.named_scope("SENT"):
-        drain(send_sem, "bc", brecv)
-        drain(send_sem, "dt", drecv)
-        drain(send_sem, "x", xrecv)
-        for c in range(n_chunk):
-            drain(send_sem, ("z", c), zrecv.at[c])
-            drain(send_sem, ("a", c), ag_v.at[c, 0:e_n])
-        drain(send_sem, "ss", ss_v.at[0:e_n])
+        drain("bc", brecv)
+        drain("dt", drecv)
+        drain("x", xrecv)
+        drain("z", zrecv)
+        drain("a", ag_v.at[:, 0:e_n])
+        drain("ss", ss_v.at[0:e_n])
         if span > 1:
-            drain(send_sem, "sq", sq_recv)
+            drain("sq", sq_recv)
 
 
 def write_kernel(n_parts, n_own, has_out, *refs):
@@ -503,20 +498,20 @@
     di = w_x.shape[1]
     hd = w_dt.shape[1]
     cols = w_out.shape[1]
-    n_own = n_heads // 2
-    fused = n_heads % 4 == 0 and n_emb % 2 == 0 and cols % (n_heads * LANES) == 0
+    n_own = n_heads
+    fused = n_heads & (n_heads - 1) == 0 and n_emb % 2 == 0 and cols % (n_heads * LANES) == 0
     chunk = min(512, di)
-    dims = (n_emb, n_heads, batch, bd, di, hd, cols, chunk, n_own, fused, span)
     n_chunk = di // chunk
+    pieces = pieces_of(n_chunk, chunk)
+    dims = (n_emb, n_heads, batch, bd, di, hd, cols, chunk, pieces, n_own, fused, span)
     vm = pl.BlockSpec(memory_space=pltpu.VMEM)
     hbm = pl.BlockSpec(memory_space=pltpu.HBM)
     dma = pltpu.SemaphoreType.DMA
     ochunk = cols // n_own if fused else LANES
     own_n = n_own if fused else 1
-    all_n = 2 * n_heads if fused else 1
     e_n = max(n_emb - 1, 1)
     q_n = max(span - 1, 1)
-    n_remote = len(GROUPS) + 2 * n_chunk
+    n_remote = len(GROUPS) - 2 + 2 * len(pieces)
     out_shape = (n_own, batch, ochunk) if fused else (batch, cols)
     out, new_state = pl.pallas_call(
         functools.partial(kernel, dims),
@@ -538,9 +533,9 @@
             pltpu.VMEM((n_chunk, depth, chunk), BF16),
             pltpu.VMEM((depth, 2 * N), BF16),
             pltpu.VMEM((hd, depth), BF16),
-            pltpu.VMEM((2, k_prev, bd, N), BF16),
-            pltpu.VMEM((2, k_prev + 1, N), F32),
-            pltpu.VMEM((n_chunk, chunk, cols), BF16),
+            pltpu.VMEM((k_prev, bd, w_bc.shape[1]), BF16),
+            pltpu.VMEM((k_prev + 1, w_bc.shape[1]), F32),
+            pltpu.VMEM((di, cols), BF16),
             pltpu.VMEM((n_emb, bd, 2 * N), F32),
             pltpu.VMEM((n_emb, bd, 2 * N), BF16),
             pltpu.VMEM((e_n, bd, 2 * N), BF16),
@@ -556,12 +551,12 @@
             pltpu.VMEM((n_chunk, n_emb, bd, chunk), BF16),
             pltpu.VMEM((n_emb, bd, LANES), F32),
             pltpu.VMEM((own_n, batch, ochunk), BF16),
-            pltpu.VMEM((all_n, batch, ochunk), BF16),
-            pltpu.VMEM((2, batch, ochunk), BF16),
+            pltpu.VMEM((own_n, batch, ochunk), BF16),
+            pltpu.VMEM((batch, ochunk), BF16),
             pltpu.VMEM((bd, LANES), F32),
             pltpu.VMEM((q_n, bd, LANES), F32),
             dma((DEPTH,)),
-            dma((n_remote,)),
+            dma((len(GROUPS),)),
             dma((n_remote,)),
         ],
         compiler_params=pltpu.CompilerParams(

time: 28.5 us -> 27.7 us (0.972)
  Pallas kernels: 27.7 us -> 26.9 us
    pallas_call x1, Pallas kernels: 24.4 us -> 23.6 us  [on_device(): pl.pallas_call(functools.partial(kernel, dims), out_shape=(pltpu.VMEM(out...]
where the time goes in v4:
time: 27.7 us; the launch traced here: 27.6 us
  Pallas kernels  26.9 us (97%)
  between operations  0.64 us (2%)
    pallas_call x1, Pallas kernels, on_device(): pl.pallas_call(functools.partial(kernel, dims), out_shape=(pltpu.VMEM(out...  23.6 us
    pallas_call x1, Pallas kernels, on_device(): pl.pallas_call(write, out_shape=(state_shape, jax.ShapeDtypeStruct((batch...  3.32 us

profile of v4, /device:TPU:0, one launch (start us, length us, event | category | flops | bytes accessed | tf_op | source)
XLA Modules:
  0.0 27.6 jit_solution(3863507799269172166)
XLA Ops:
  0.6 23.6 %shard_map.158 = (bf16[8,16,256]{2,1,0:T(8,128)(2,1)S(1)}, f32[4,2048,256]{2,1,0:T(8,128)S(1)}) custom-call(bf16[16,2048]{1,0:T(8,128)(2,1)} %hidden_hbm.1, f32[1,32]{1,0:T(1,128)} %bitcast.14, f32[1,32]{1,0:T(1,128)} %bitcast.15, f32[1,32]{1,0:T(1,128)} %bitcast.16, bf16[3,4,2048]{2,1,0:T(4,128)(2,1)} %bitcast.12, f32[4,2048]{1,0:T(4,128)} %convwx_hbm.1, ...), custom_call_target="tpu_custom_call" | custom-call | tf_op jit(solution)/shard_map/pallas_call | solution.py:516
  24.3 3.3 %shard_map.159 = (f32[4,2048,256]{2,1,0:T(8,128)}, bf16[16,2048]{1,0:T(8,128)(2,1)}) custom-call(f32[4,2048,256]{2,1,0:T(8,128)S(1)} %get-tuple-element.6.refs_0_, bf16[8,16,256]{2,1,0:T(8,128)(2,1)S(1)} %get-tuple-element.7.refs_1_), custom_call_target="tpu_custom_call" | custom-call | tf_op jit(solution)/shard_map/pallas_call | solution.py:590

commit v5 on v4

--- a/solution.py
+++ b/solution.py
@@ -12,7 +12,7 @@
 N = 256
 G = 8
 LANES = 128
-DEPTH = 18
+DEPTH = 14
 GROUPS = ("bc", "dt", "x", "ss", "sq", "rs", "ag", "z", "a")
 MESH = pl.DeviceIdType.MESH
 F32 = jnp.float32
@@ -105,6 +105,7 @@
     group = h // span
     n_chunk = di // chunk
     e_n = n_emb - 1
+    depth = hidden_ref.shape[1]
     core = lax.rem(e, 2)
     partner = e + 1 - 2 * core
 
@@ -135,8 +136,11 @@
     stream("dt", wdt_hbm, wdt_v)
     for c in range(n_chunk):
         stream(("x", c), wx_hbm.at[:, pl.ds(c * chunk, chunk)], wx_v.at[c])
+    z_cuts = [1] * (n_chunk - 1) + [2]
     for c in range(n_chunk):
-        stream(("z", c), wz_hbm.at[:, pl.ds(c * chunk, chunk)], wz_v.at[c])
+        for k in range(z_cuts[c]):
+            rows = pl.ds(k * depth // z_cuts[c], depth // z_cuts[c])
+            stream(("z", c, k), wz_hbm.at[rows, pl.ds(c * chunk, chunk)], wz_v.at[c, rows])
     stream("cb", convbc_hbm, convbc_v)
     stream("cw", convwbc_hbm, convwbc_v)
     stream("dtb", dtb_hbm, dtb_ref)
@@ -233,8 +237,7 @@
     ready("hidden")
     hidden = hidden_ref[...]
 
-    def project(weights, own, out):
-        part = jnp.dot(hidden, weights, preferred_element_type=F32)
+    def project(part, own, out):
         for peer in range(n_emb):
             mine = part[peer * bd : (peer + 1) * bd]
             own[peer] = mine
@@ -247,7 +250,7 @@
 
     for half in range(2):
         ready(("bc", half))
-    project(wbc_v[...], bpart, bsend)
+    project(jnp.dot(hidden, wbc_v[...], preferred_element_type=F32), bpart, bsend)
     ready("dt")
     dsend[...] = jnp.zeros(dsend.shape, F32)
     part = lax.dot_general(
@@ -259,7 +262,8 @@
     greet_at = min(2, n_chunk - 1)
     for c in range(n_chunk):
         ready(("x", c))
-        project(wx_v[c], xpart.at[c], xsend.at[c])
+        part = jnp.dot(hidden, wx_v[c], preferred_element_type=F32)
+        project(part, xpart.at[c], xsend.at[c])
         if c == greet_at:
             with jax.named_scope("BARRIER"):
                 pl.semaphore_wait(barrier, n_greet)
@@ -269,8 +273,13 @@
             send_emb("x", lambda peer, k=k: xsend.at[k, peer], lambda o, k=k: xrecv.at[k, o])
 
     def do_z(c):
-        ready(("z", c))
-        project(wz_v[c], zpart.at[c], zsend.at[c])
+        part = None
+        for k in range(z_cuts[c]):
+            rows = slice(k * depth // z_cuts[c], (k + 1) * depth // z_cuts[c])
+            ready(("z", c, k))
+            more = jnp.dot(hidden[:, rows], wz_v[c, rows], preferred_element_type=F32)
+            part = more if part is None else part + more
+        project(part, zpart.at[c], zsend.at[c])
         send_emb(("z", c), lambda peer: zsend.at[c, peer], lambda o: zrecv.at[c, o])
 
     def total_of(own, got):
@@ -349,11 +358,13 @@
         cols_v[here, :] = jnp.transpose(rows)
 
         def step_of(j, carry):
-            at = pl.ds(pl.multiple_of(c * chunk + j * rows_at, rows_at), rows_at)
-            for b in range(bd):
-                xcol = cols_v[at, b : b + 1]
-                dcol = cols_v[at, bd + b : bd + b + 1]
-                st_ref[b, at, :] = dcol * st_ref[b, at, :] + xcol * b_group[b : b + 1, :]
+            for k in range(rows_at // P_SIZE):
+                first = pl.multiple_of(c * chunk + j * rows_at + k * P_SIZE, P_SIZE)
+                at = pl.ds(first, P_SIZE)
+                for b in range(bd):
+                    xcol = cols_v[at, b : b + 1]
+                    rate = jnp.broadcast_to(cols_v[pl.ds(first, 1), bd + b : bd + b + 1], (1, N))
+                    st_ref[b, at, :] = rate * st_ref[b, at, :] + xcol * b_group[b : b + 1, :]
             return carry
 
         with jax.named_scope("UPD"):
@@ -370,12 +381,15 @@
         for o in range(e_n):
             z_all = z_all + zrecv[c, o, :, here].astype(F32)
         gated = (decay_c[:, at] * raw + adds[c][:, here]) * silu(z_all)
-        ag_v[c, e, :, here] = (gated * gain_ref[:, at]).astype(BF16)
-        spread(("a", p), ag_v.at[c, e, :, here])
         for lane in range(0, width, LANES):
             squares = gated[:, lane : lane + LANES]
             squares = squares * squares
             total = squares if total is None else total + squares
+        if span == 1 and p == len(pieces) - 1:
+            ss_v[e] = total
+            spread("ss", ss_v.at[e])
+        ag_v[c, e, :, here] = (gated * gain_ref[:, at]).astype(BF16)
+        spread(("a", p), ag_v.at[c, e, :, here])
     if span > 1:
         sq_send[...] = total
         for o in range(1, span):
@@ -384,10 +398,10 @@
         arrived("sq", sq_recv)
         for o in range(span - 1):
             total = total + sq_recv[o]
-    ss_v[e] = total
-    spread("ss", ss_v.at[e])
-
-    late = n_chunk // 4
+        ss_v[e] = total
+        spread("ss", ss_v.at[e])
+
+    late = n_chunk // 2
     for c in range(late):
         update(c)
 
@@ -398,14 +412,15 @@
         whole = jnp.concatenate(
             [ag_v[c, i, :, here].astype(F32) for i in range(n_emb)], axis=0
         ).astype(BF16)
+        if p == len(pieces) - 1:
+            arrived("ss", ss_v.at[0:e_n])
+            sums = jnp.concatenate([ss_v[i] for i in range(n_emb)], axis=0)
+            sums = jnp.sum(sums, axis=1, keepdims=True)
+            inv_rms = lax.rsqrt(sums / (H * P_SIZE // G) + 1e-05)
         ready(("o", p))
         weights = wout_v[c * chunk + lo : c * chunk + lo + width]
         part = jnp.dot(whole, weights, preferred_element_type=F32)
         acc = part if acc is None else acc + part
-    arrived("ss", ss_v.at[0:e_n])
-    sums = jnp.concatenate([ss_v[i] for i in range(n_emb)], axis=0)
-    sums = jnp.sum(sums, axis=1, keepdims=True)
-    inv_rms = lax.rsqrt(sums / (H * P_SIZE // G) + 1e-05)
     acc = acc * inv_rms
     if not fused:
         out_ref[...] = acc
@@ -419,7 +434,7 @@
             peer = head_peer(m)
             send("rs", rs_send.at[peer], rs_recv.at[m], {"emb": partner, "heads": peer})
 
-        for c in range(late, 2 * late):
+        for c in range(late, n_chunk):
             update(c)
 
         arrived("rs", rs_recv)
@@ -429,8 +444,6 @@
         fin_send[...] = whole_sum.astype(BF16)
         for peer in range(n_own):
             send("ag", fin_send, out_ref.at[h], {"emb": partner, "heads": peer})
-        for c in range(2 * late, n_chunk):
-            update(c)
         arrived("ag", out_ref)
         drain("rs", rs_send)
         drain("ag", rs_recv)

time: 27.7 us -> 27.7 us (level)
  no operation moved by 1% of the time
where the time goes in v5:
time: 27.7 us; the launch traced here: 27.6 us
  Pallas kernels  26.9 us (97%)
  between operations  0.64 us (2%)
    pallas_call x1, Pallas kernels, on_device(): pl.pallas_call(functools.partial(kernel, dims), out_shape=(pltpu.VMEM(out...  23.6 us
    pallas_call x1, Pallas kernels, on_device(): pl.pallas_call(write, out_shape=(state_shape, jax.ShapeDtypeStruct((batch...  3.32 us

profile of v5, /device:TPU:0, one launch (start us, length us, event | category | flops | bytes accessed | tf_op | source)
XLA Modules:
  0.0 27.6 jit_solution(4467087043916546350)
XLA Ops:
  0.6 23.6 %shard_map.158 = (bf16[8,16,256]{2,1,0:T(8,128)(2,1)S(1)}, f32[4,2048,256]{2,1,0:T(8,128)S(1)}) custom-call(bf16[16,2048]{1,0:T(8,128)(2,1)} %hidden_hbm.1, f32[1,32]{1,0:T(1,128)} %bitcast.14, f32[1,32]{1,0:T(1,128)} %bitcast.15, f32[1,32]{1,0:T(1,128)} %bitcast.16, bf16[3,4,2048]{2,1,0:T(4,128)(2,1)} %bitcast.12, f32[4,2048]{1,0:T(4,128)} %convwx_hbm.1, ...), custom_call_target="tpu_custom_call" | custom-call | tf_op jit(solution)/shard_map/pallas_call | solution.py:529
  24.3 3.3 %shard_map.159 = (f32[4,2048,256]{2,1,0:T(8,128)}, bf16[16,2048]{1,0:T(8,128)(2,1)}) custom-call(f32[4,2048,256]{2,1,0:T(8,128)S(1)} %get-tuple-element.6.refs_0_, bf16[8,16,256]{2,1,0:T(8,128)(2,1)S(1)} %get-tuple-element.7.refs_1_), custom_call_target="tpu_custom_call" | custom-call | tf_op jit(solution)/shard_map/pallas_call | solution.py:603

commit v6 on v5

--- a/solution.py
+++ b/solution.py
@@ -13,7 +13,8 @@
 G = 8
 LANES = 128
 DEPTH = 14
-GROUPS = ("bc", "dt", "x", "ss", "sq", "rs", "ag", "z", "a")
+GROUPS = ("bc", "dt", "x", "ss", "rs", "ag", "z", "a", "sq")
+BASE = 6
 MESH = pl.DeviceIdType.MESH
 F32 = jnp.float32
 BF16 = jnp.bfloat16
@@ -199,9 +200,13 @@
         return GROUPS.index(name if isinstance(name, str) else name[0])
 
     def got_at(name):
+        if name == "sq":
+            return BASE + n_chunk + len(pieces)
         if isinstance(name, str):
             return GROUPS.index(name)
-        return len(GROUPS) - 2 + 2 * name[1] + (name[0] == "z")
+        if name[0] == "z":
+            return BASE + name[1]
+        return BASE + n_chunk + name[1]
 
     def send(name, src, dst, where):
         pltpu.make_async_remote_copy(
@@ -237,11 +242,13 @@
     ready("hidden")
     hidden = hidden_ref[...]
 
-    def project(part, own, out):
+    def project(part, own, out, go=None):
         for peer in range(n_emb):
-            mine = part[peer * bd : (peer + 1) * bd]
-            own[peer] = mine
-            out[peer] = mine.astype(BF16)
+            out[peer] = part[peer * bd : (peer + 1) * bd].astype(BF16)
+        if go is not None:
+            go()
+        for peer in range(n_emb):
+            own[peer] = part[peer * bd : (peer + 1) * bd]
 
     k_prev = convx_v.shape[0]
 
@@ -279,8 +286,12 @@
             ready(("z", c, k))
             more = jnp.dot(hidden[:, rows], wz_v[c, rows], preferred_element_type=F32)
             part = more if part is None else part + more
-        project(part, zpart.at[c], zsend.at[c])
-        send_emb(("z", c), lambda peer: zsend.at[c, peer], lambda o: zrecv.at[c, o])
+        project(
+            part,
+            zpart.at[c],
+            zsend.at[c],
+            lambda: send_emb(("z", c), lambda peer: zsend.at[c, peer], lambda o: zrecv.at[c, o]),
+        )
 
     def total_of(own, got):
         value = own[e]
@@ -401,7 +412,7 @@
         ss_v[e] = total
         spread("ss", ss_v.at[e])
 
-    late = n_chunk // 2
+    late = n_chunk // 4
     for c in range(late):
         update(c)
 
@@ -430,7 +441,7 @@
         ochunk = cols // n_own
         for j in range(n_own):
             rs_send[j] = acc[:, j * ochunk : (j + 1) * ochunk].astype(BF16)
-        for m in range(n_own - 1, -1, -1):
+        for m in [*range(n_own - 3, 0, -1), n_own - 2, n_own - 1, 0]:
             peer = head_peer(m)
             send("rs", rs_send.at[peer], rs_recv.at[m], {"emb": partner, "heads": peer})
 
@@ -442,7 +453,7 @@
         for m in range(1, n_own):
             whole_sum = whole_sum + rs_recv[m].astype(F32)
         fin_send[...] = whole_sum.astype(BF16)
-        for peer in range(n_own):
+        for peer in [0, 1, *range(n_own - 1, 1, -1)]:
             send("ag", fin_send, out_ref.at[h], {"emb": partner, "heads": peer})
         arrived("ag", out_ref)
         drain("rs", rs_send)
@@ -524,7 +535,8 @@
     own_n = n_own if fused else 1
     e_n = max(n_emb - 1, 1)
     q_n = max(span - 1, 1)
-    n_remote = len(GROUPS) - 2 + 2 * len(pieces)
+    more = int(span > 1)
+    n_remote = BASE + n_chunk + len(pieces) + more
     out_shape = (n_own, batch, ochunk) if fused else (batch, cols)
     out, new_state = pl.pallas_call(
         functools.partial(kernel, dims),
@@ -569,7 +581,7 @@
             pltpu.VMEM((bd, LANES), F32),
             pltpu.VMEM((q_n, bd, LANES), F32),
             dma((DEPTH,)),
-            dma((len(GROUPS),)),
+            dma((BASE + 2 + more,)),
             dma((n_remote,)),
         ],
         compiler_params=pltpu.CompilerParams(
@@ -594,7 +606,7 @@
             w_out,
         )
     )
-    n_parts = max(di // 512, 1)
+    n_parts = max(di // 128, 1)
     params = pltpu.CompilerParams(vmem_limit_bytes=2 * 1024 * 1024)
     sems = dma((2,))
     state_shape = jax.ShapeDtypeStruct((bd, di, N), F32)

time: 27.7 us -> 27.1 us (0.978)
  Pallas kernels: 26.9 us -> 26.3 us
    pallas_call x1, Pallas kernels: 23.6 us -> 23 us  [on_device(): pl.pallas_call(functools.partial(kernel, dims), out_shape=(pltpu.VMEM(out...]
where the time goes in v6:
time: 27.1 us; the launch traced here: 27 us
  Pallas kernels  26.3 us (97%)
  between operations  0.64 us (2%)
    pallas_call x1, Pallas kernels, on_device(): pl.pallas_call(functools.partial(kernel, dims), out_shape=(pltpu.VMEM(out...  23 us
    pallas_call x1, Pallas kernels, on_device(): pl.pallas_call(write, out_shape=(state_shape, jax.ShapeDtypeStruct((batch...  3.28 us

profile of v6, /device:TPU:0, one launch (start us, length us, event | category | flops | bytes accessed | tf_op | source)
XLA Modules:
  0.0 27.0 jit_solution(4477815251864869274)
XLA Ops:
  0.6 23.0 %shard_map.158 = (bf16[8,16,256]{2,1,0:T(8,128)(2,1)S(1)}, f32[4,2048,256]{2,1,0:T(8,128)S(1)}) custom-call(bf16[16,2048]{1,0:T(8,128)(2,1)} %hidden_hbm.1, f32[1,32]{1,0:T(1,128)} %bitcast.14, f32[1,32]{1,0:T(1,128)} %bitcast.15, f32[1,32]{1,0:T(1,128)} %bitcast.16, bf16[3,4,2048]{2,1,0:T(4,128)(2,1)} %bitcast.12, f32[4,2048]{1,0:T(4,128)} %convwx_hbm.1, ...), custom_call_target="tpu_custom_call" | custom-call | tf_op jit(solution)/shard_map/pallas_call | solution.py:541
  23.7 3.3 %shard_map.159 = (f32[4,2048,256]{2,1,0:T(8,128)}, bf16[16,2048]{1,0:T(8,128)(2,1)}) custom-call(f32[4,2048,256]{2,1,0:T(8,128)S(1)} %get-tuple-element.6.refs_0_, bf16[8,16,256]{2,1,0:T(8,128)(2,1)S(1)} %get-tuple-element.7.refs_1_), custom_call_target="tpu_custom_call" | custom-call | tf_op jit(solution)/shard_map/pallas_call | solution.py:615

commit v7 on v6

--- a/solution.py
+++ b/solution.py
@@ -453,7 +453,7 @@
         for m in range(1, n_own):
             whole_sum = whole_sum + rs_recv[m].astype(F32)
         fin_send[...] = whole_sum.astype(BF16)
-        for peer in [0, 1, *range(n_own - 1, 1, -1)]:
+        for peer in [0, 1, *range(n_own - 1, 1, -2), *range(n_own - 2, 1, -2)]:
             send("ag", fin_send, out_ref.at[h], {"emb": partner, "heads": peer})
         arrived("ag", out_ref)
         drain("rs", rs_send)
@@ -475,18 +475,18 @@
         st_v, fin_v, st_hbm, out_hbm, sem = refs
     else:
         st_v, st_hbm, sem = refs
+    bd, di, _ = st_v.shape
+    rows = di // n_parts
+    for b in range(bd):
+        for i in range(n_parts):
+            part = pl.ds(i * rows, rows)
+            pltpu.make_async_copy(st_v.at[b, part], st_hbm.at[b, part], sem.at[0]).start()
     if has_out:
         ochunk = fin_v.shape[2]
         for i in range(n_own):
             pltpu.make_async_copy(
                 fin_v.at[i], out_hbm.at[:, i * ochunk : (i + 1) * ochunk], sem.at[1]
             ).start()
-    bd, di, _ = st_v.shape
-    rows = di // n_parts
-    for b in range(bd):
-        for i in range(n_parts):
-            part = pl.ds(i * rows, rows)
-            pltpu.make_async_copy(st_v.at[b, part], st_hbm.at[b, part], sem.at[0]).start()
     if has_out:
         pltpu.make_async_copy(fin_v, fin_v, sem.at[1]).wait()
     pltpu.make_async_copy(st_v, st_hbm, sem.at[0]).wait()

time: 27.1 us -> 27.1 us (level)
  no operation moved by 1% of the time
where the time goes in v7:
time: 27.1 us; the launch traced here: 27 us
  Pallas kernels  26.3 us (97%)
  between operations  0.64 us (2%)
    pallas_call x1, Pallas kernels, on_device(): pl.pallas_call(functools.partial(kernel, dims), out_shape=(pltpu.VMEM(out...  23 us
    pallas_call x1, Pallas kernels, on_device(): pl.pallas_call(write, out_shape=(state_shape, jax.ShapeDtypeStruct((batch...  3.26 us

profile of v7, /device:TPU:0, one launch (start us, length us, event | category | flops | bytes accessed | tf_op | source)
XLA Modules:
  0.0 27.0 jit_solution(3517670292443202920)
XLA Ops:
  0.6 23.0 %shard_map.158 = (bf16[8,16,256]{2,1,0:T(8,128)(2,1)S(1)}, f32[4,2048,256]{2,1,0:T(8,128)S(1)}) custom-call(bf16[16,2048]{1,0:T(8,128)(2,1)} %hidden_hbm.1, f32[1,32]{1,0:T(1,128)} %bitcast.14, f32[1,32]{1,0:T(1,128)} %bitcast.15, f32[1,32]{1,0:T(1,128)} %bitcast.16, bf16[3,4,2048]{2,1,0:T(4,128)(2,1)} %bitcast.12, f32[4,2048]{1,0:T(4,128)} %convwx_hbm.1, ...), custom_call_target="tpu_custom_call" | custom-call | tf_op jit(solution)/shard_map/pallas_call | solution.py:541
  23.7 3.3 %shard_map.159 = (f32[4,2048,256]{2,1,0:T(8,128)}, bf16[16,2048]{1,0:T(8,128)(2,1)}) custom-call(f32[4,2048,256]{2,1,0:T(8,128)S(1)} %get-tuple-element.6.refs_0_, bf16[8,16,256]{2,1,0:T(8,128)(2,1)S(1)} %get-tuple-element.7.refs_1_), custom_call_target="tpu_custom_call" | custom-call | tf_op jit(solution)/shard_map/pallas_call | solution.py:615
